TPU v7x, 256 devices: a whole 4x4x8 slice. The times are simulated.
256 devices in a mesh: patch: 32 (over x, z_hi, core), tp: 8 (over y, z_lo).
Axes of the slice: x: 4, y: 4, z: 8 (z_hi: 4, z_lo: 2; z = z_hi * 2 + z_lo), core: 2. Of those that a mesh axis runs over, the one named last changes fastest.
Arguments:
- resid_corrupt: bfloat16 [512, 4096], P(None, 'tp'), may hold values from -6 to 6
- resid_clean: bfloat16 [2, 512, 4096], P(None, 'patch', 'tp'), may hold values from -6 to 6
- patch_level: int32 [32], P('patch'), may hold values from 0 to 1
- patch_mask: int32 [32, 128], P('patch'), may hold values 0 or 1
- norm_gain: bfloat16 [4096], P('tp'), may hold values from 0.099609375 to 1.8984375
- final_gain: bfloat16 [4096], P('tp'), may hold values from 0.099609375 to 1.8984375
- w_query: bfloat16 [4096, 4096], P('patch', 'tp'), may hold values from -1 to 1
- w_key: bfloat16 [4096, 1024], P('patch', 'tp'), may hold values from -1 to 1
- w_value: bfloat16 [4096, 1024], P('patch', 'tp'), may hold values from -0.09375 to 0.09375
- w_out: bfloat16 [4096, 4096], P('tp', 'patch'), may hold values from -0.09375 to 0.09375
- unembed: bfloat16 [128256, 4096], P(('patch', 'tp')), may hold values from -0.09375 to 0.09375
- scored_ids: int32 [256], replicated, may hold values from 0 to 128255
- base_logits: float32 [512, 256], P('tp'), may hold values from -6 to 6
Outputs:
- logit_shift: float32 [32, 512, 256], P('patch', 'tp')
All inputs are finite; a program needn't handle non-finite values. No bound on the sum of `patch_mask` on one device may be relied on, other than what follows from the above.
Results may differ from a plain program's by a relative error of at most 0.01.
The roundings to bfloat16 on the way count: a program that leaves them out, or rounds other values in their place, can miss the bound.
Values may be sent and summed in bfloat16 or wider, within the bound.
A program may use at most 128 MiB of HBM per device.

v0:
```python
import jax
import jax.numpy as jnp
from jax import lax
from jax.sharding import PartitionSpec as P

D = 4096
HD = 128
SEQ = 128
PROMPTS = 4


EPSILON = 1e-05
THETA = 500000.0


def in_one_piece(arrays, axis, dim, along):
    both = jnp.concatenate(arrays, axis=along)
    out, at, gathered = (lax.all_gather(both, axis, axis=dim, tiled=True), 0, [])
    for a in arrays:
        gathered.append(lax.slice_in_dim(out, at, at + a.shape[along], axis=along))
        at += a.shape[along]
    return tuple(gathered)


def in_blocks(value, dim, peers):
    dims = value.shape
    pieces = value.reshape(*dims[:dim], peers, dims[dim] // peers, *dims[dim + 1 :])
    return jnp.moveaxis(pieces, dim, 0)


def summed_on_arrival(value, axis, dim):
    pieces = in_blocks(value, dim, lax.axis_size(axis))
    arrived = lax.all_to_all(pieces, axis, split_axis=0, concat_axis=0, tiled=True)
    return arrived.astype(jnp.float32).sum(axis=0)


def total_of_pieces(value, axis):
    pieces = lax.all_gather(value, axis).astype(jnp.float32)
    return pieces.sum(axis=0)


def rope_tables(length, head_dim):
    half = head_dim // 2
    freqs = THETA ** (-(jnp.arange(half, dtype=jnp.float32) * 2.0 / head_dim))
    angles = jnp.arange(length, dtype=jnp.float32)[:, None] * freqs[None, :]
    return (jnp.cos(angles)[:, None, :], jnp.sin(angles)[:, None, :])


def rotate(values, cosine, sine):
    half = values.shape[-1] // 2
    lower = values[..., :half]
    upper = values[..., half:]
    return jnp.concatenate([lower * cosine - upper * sine, upper * cosine + lower * sine], axis=-1)


def rms_scale(rows, gain):
    return rows * lax.rsqrt(jnp.mean(rows * rows, axis=-1, keepdims=True) + EPSILON) * gain


def attend(query_f, key_f, value_f):
    heads = query_f.shape[1] // HD
    kv_heads = key_f.shape[1] // HD
    group = heads // kv_heads
    prompts = query_f.shape[0] // SEQ
    cosine, sine = rope_tables(SEQ, HD)
    queries = rotate(query_f.reshape(prompts, SEQ, heads, HD), cosine, sine).astype(jnp.bfloat16)
    queries = queries.reshape(prompts, SEQ, kv_heads, group, HD)
    key_rows = rotate(key_f.reshape(prompts, SEQ, kv_heads, HD), cosine, sine).astype(jnp.bfloat16)
    value_rows = value_f.astype(jnp.bfloat16).reshape(prompts, SEQ, kv_heads, HD)
    scores = jnp.einsum(
        "pqkgd,pskd->pkgqs", queries, key_rows, preferred_element_type=jnp.float32
    ) * HD ** (-0.5)
    causal = lax.iota(jnp.int32, SEQ)[:, None] >= lax.iota(jnp.int32, SEQ)[None, :]
    scores = jnp.where(causal, scores, -1e30)
    probs = jax.nn.softmax(scores, axis=-1).astype(jnp.bfloat16)
    attended = jnp.einsum(
        "pkgqs,pskd->pqkgd", probs, value_rows, preferred_element_type=jnp.float32
    )
    return attended.astype(jnp.bfloat16).reshape(prompts * SEQ, heads * HD)


def on_device(
    resid_corrupt,
    resid_clean,
    patch_level,
    patch_mask,
    norm_gain,
    final_gain,
    w_query,
    w_key,
    w_value,
    w_out,
    unembed,
    scored_ids,
    base_logits,
):
    level = patch_level[0]
    row_mask = jnp.tile(patch_mask[0], PROMPTS) == 1
    clean_all = lax.all_gather(resid_clean, "patch", axis=1, tiled=True)
    early = (row_mask & (level == 0))[:, None]
    layer_in = jnp.where(early, clean_all[0], resid_corrupt)
    full_rows, full_gain = (
        lax.all_gather(layer_in, "tp", axis=1, tiled=True),
        lax.all_gather(norm_gain, "tp", axis=0, tiled=True),
    )
    normed = rms_scale(full_rows.astype(jnp.float32), full_gain.astype(jnp.float32)).astype(
        jnp.bfloat16
    )
    pieces = in_one_piece((w_query, w_key, w_value), "patch", 0, 1)
    query_f = jnp.dot(normed, pieces[0], preferred_element_type=jnp.float32)
    key_f = jnp.dot(normed, pieces[1], preferred_element_type=jnp.float32)
    value_f = jnp.dot(normed, pieces[2], preferred_element_type=jnp.float32)
    attended = attend(query_f, key_f, value_f)
    partial_out = jnp.dot(
        attended,
        lax.all_gather(w_out, "patch", axis=1, tiled=True),
        preferred_element_type=jnp.float32,
    )
    head_block = summed_on_arrival(partial_out.astype(jnp.bfloat16), "tp", 1)
    middle = layer_in.astype(jnp.float32) + head_block
    late = (row_mask & (level == 1))[:, None]
    residual = jnp.where(late, clean_all[1].astype(jnp.float32), middle)
    squares = lax.psum(jnp.sum(residual * residual, axis=1), "tp")
    scaling = lax.rsqrt(squares / D + EPSILON)[:, None]
    final_block = (residual * scaling * final_gain.astype(jnp.float32)).astype(jnp.bfloat16)
    rows_dev = unembed.shape[0]
    first_row = lax.axis_index(("patch", "tp")) * rows_dev
    owned_rows = (scored_ids[:, None] == first_row + lax.iota(jnp.int32, rows_dev)[None, :]).astype(
        jnp.bfloat16
    )
    picked = jnp.dot(owned_rows, unembed, preferred_element_type=jnp.float32)
    spread = summed_on_arrival(picked.astype(jnp.bfloat16), "tp", 1)
    score_block = (
        total_of_pieces(spread.astype(jnp.bfloat16), "patch")
        .astype(jnp.float32)
        .astype(jnp.bfloat16)
    )
    partial_logits = jnp.einsum(
        "td,sd->ts", final_block, score_block, preferred_element_type=jnp.float32
    )
    token_logits = summed_on_arrival(partial_logits.astype(jnp.bfloat16), "tp", 0)
    return (token_logits - base_logits)[None]


def solution(mesh):
    placed = (
        P(None, "tp"),
        P(None, "patch", "tp"),
        P("patch"),
        P("patch", None),
        P("tp"),
        P("tp"),
        P("patch", "tp"),
        P("patch", "tp"),
        P("patch", "tp"),
        P("tp", "patch"),
        P(("patch", "tp"), None),
        P(),
        P("tp", None),
    )
    return jax.shard_map(
        on_device, mesh=mesh, in_specs=placed, out_specs=P("patch", "tp", None), check_vma=False
    )
```

profile of v0, /device:TPU:2, one launch (start us, length us, event | category | flops | bytes accessed | tf_op | source)
XLA Modules:
  0.0 461.8 jit_solution(4920440208380993172)
XLA Ops:
  6.5 0.7 all-gather.8.cloned.1.call-update
  8.0 0.7 and_bitcast_fusion.1
  8.6 55.1 %all-gather.8.cloned.1.call-done = bf16[2,512,512]{2,1,0:T(8,128)(2,1)} async-done(((bf16[2,16,512]{2,1,0:T(8,128)(2,1)}), bf16[2,512,512]{2,1,0:T(8,128)(2,1)}) %all-gather.8.cloned.1.call-update) | async-done | bytes 1048592 | tf_op jit(solution)/shard_map/all_gather | solution.py:99
  63.7 2.1 fusion.14
  65.9 1.7 pad_maximum_fusion
  67.6 0.5 all-gather.14.cloned.1.call-update
  68.2 3.5 convolution_convert_fusion.1
  72.0 54.5 %all_to_all.15 = bf16[8,256,512]{2,1,0:T(8,128)(2,1)S(1)} all-to-all(bf16[8,256,512]{2,1,0:T(8,128)(2,1)S(1)} %bitcast.85), channel_id=1, replica_groups=mesh['patch'=32,'tp'=8] {'tp'}, dimensions={0} | all-to-all | bytes 4194304 | tf_op jit(solution)/shard_map/all_to_all | solution.py:33
  126.5 1.1 reduce_sum.73
  127.6 25.7 %all-gather.1 = bf16[8,1,512]{2,1,0:T(2,128)(2,1)S(1)} all-gather(bf16[1,1,512]{2,1,0:T(2,128)(2,1)S(1)} %reshape.154), channel_id=1, replica_groups=mesh['patch'=32,'tp'=8] {'tp'}, dimensions={0}, use_global_device_ids=true | all-gather | bytes 9216 | tf_op jit(solution)/shard_map/all_gather | solution.py:104
  153.6 27.4 %all-gather.10.cloned.1.call-done = bf16[512,4096]{1,0:T(8,128)(2,1)} async-done(((bf16[512,512]{1,0:T(8,128)(2,1)}), bf16[512,4096]{1,0:T(8,128)(2,1)}) %all-gather.10.cloned.1.call-update) | async-done | bytes 4194320 | tf_op jit(solution)/shard_map/all_gather | solution.py:103
  181.0 3.1 fusion
  184.1 67.0 %all-gather.12.cloned.1.call-done = bf16[4096,768]{1,0:T(8,128)(2,1)} async-done(((bf16[128,768]{1,0:T(8,128)(2,1)}), bf16[4096,768]{1,0:T(8,128)(2,1)}) %all-gather.12.cloned.1.call-update) | async-done | bytes 6291472 | tf_op jit(solution)/shard_map/all_gather | solution.py:18
  251.1 5.8 %fusion.3 = f32[512,512]{1,0:T(8,128)S(1)} fusion(bf16[4096,768]{1,0:T(8,128)(2,1)} %all-gather.12.cloned.1.call-done, bf16[512,4096]{1,0:T(8,128)(2,1)} %all-gather.10.cloned.1.call-done, f32[4096]{0:T(1024)S(1)} %bitcast.91, f32[512]{0:T(512)S(1)} %add_rsqrt_fusion.1), kind=kOutput, calls=%fused_computation.9 | convolution fusion | flops 2155872256 | bytes 9455616 | tf_op jit(solution)/shard_map/dot_general | solution.py:110
  257.0 0.4 reshape.146
  257.3 3.8 fusion.8
  261.3 0.6 fusion.34
  262.2 0.5 fusion.35
  262.9 1.2 copy-done.1
  264.1 2.6 convolution_convert_fusion.4
  267.4 48.2 %all-gather.14.cloned.1.call-done = bf16[512,4096]{1,0:T(8,128)(2,1)} async-done(((bf16[512,128]{1,0:T(8,128)(2,1)}), bf16[512,4096]{1,0:T(8,128)(2,1)}) %all-gather.14.cloned.1.call-update) | async-done | bytes 4194320 | tf_op jit(solution)/shard_map/all_gather | solution.py:116
  315.5 4.5 convolution_convert_fusion
  320.1 2.3 copy.57
  322.4 5.0 %all-to-all-start = ((bf16[8,512,512]{2,1,0:T(8,128)(2,1)}), bf16[8,512,512]{2,1,0:T(8,128)(2,1)}, u32[]{:S(2)}, u32[]{:S(2)}) async-start(bf16[8,512,512]{2,1,0:T(8,128)(2,1)} %bitcast.83), calls=%async_computation | async-start | bytes 8388608 | tf_op jit(solution)/shard_map/all_to_all | solution.py:33
  327.4 92.0 %all-to-all-done = bf16[8,512,512]{2,1,0:T(8,128)(2,1)} async-done(((bf16[8,512,512]{2,1,0:T(8,128)(2,1)}), bf16[8,512,512]{2,1,0:T(8,128)(2,1)}, u32[]{:S(2)}, u32[]{:S(2)}) %all-to-all-start) | async-done | bytes 4194336 | tf_op jit(solution)/shard_map/all_to_all | solution.py:33
  419.5 2.9 convert_reduce_fusion
  422.4 0.4 multiply_reduce_fusion
  422.7 16.9 %psum.7 = f32[512]{0:T(512)S(1)} all-reduce(f32[512]{0:T(512)S(1)} %multiply_reduce_fusion), channel_id=1, replica_groups=mesh['patch'=32,'tp'=8] {'tp'}, use_global_device_ids=true, to_apply=%region_5.6 | all-reduce | flops 512 | bytes 4096 | tf_op jit(solution)/shard_map/psum | solution.py:123
  439.6 4.8 %reduce_sum.74 = bf16[256,512]{1,0:T(8,128)(2,1)S(1)} reduce(bf16[32,256,512]{2,1,0:T(8,128)(2,1)} %bitcast.84, bf16[]{:T(256)} %constant.47.clone.1), dimensions={0}, to_apply=%region_7.8 | reduce | flops 4063232 | bytes 8650754 | tf_op jit(solution)/shard_map/reduce_sum | solution.py:39
  444.4 0.4 convolution_convert_fusion.3
  444.9 9.7 %all_to_all.16 = bf16[8,64,256]{2,1,0:T(8,128)(2,1)S(1)} all-to-all(bf16[8,64,256]{2,1,0:T(8,128)(2,1)S(1)} %bitcast.90), channel_id=1, replica_groups=mesh['patch'=32,'tp'=8] {'tp'}, dimensions={0} | all-to-all | bytes 524288 | tf_op jit(solution)/shard_map/all_to_all | solution.py:33
  454.6 0.6 subtract_bitcast_fusion
  (38 shorter events, 2.1 us)
Async XLA Ops:
  6.5 57.2 %all-gather.8.cloned.1.call-start = ((), (), s32[]{:S(2)}) async-start(), calls=%async_computation.3 | async-start | bytes 1081344 | tf_op jit(solution)/shard_map/all_gather | solution.py:99
  7.3 173.8 %all-gather.10.cloned.1.call-start = ((), (), s32[]{:S(2)}) async-start(), calls=%async_computation.4 | async-start | bytes 4718592 | tf_op jit(solution)/shard_map/all_gather | solution.py:103
  65.9 185.3 %all-gather.12.cloned.1.call-start = ((), (), s32[]{:S(2)}) async-start(), calls=%async_computation.5 | async-start | bytes 6488064 | tf_op jit(solution)/shard_map/all_gather | solution.py:18
  67.6 247.9 %all-gather.14.cloned.1.call-start = ((), (), s32[]{:S(2)}) async-start(), calls=%async_computation.6 | async-start | bytes 4325376 | tf_op jit(solution)/shard_map/all_gather | solution.py:116
  68.2 371.4 %all-gather.16.cloned.1.call-start = ((), (), s32[]{:S(2)}) async-start(), calls=%async_computation.7 | async-start | bytes 8650752 | tf_op jit(solution)/shard_map/all_gather | solution.py:38
  72.0 55.6 %copy-start.4 = (bf16[512]{0:T(512)(128)(2,1)S(1)}, bf16[512]{0:T(512)(128)(2,1)}, u32[]{:S(2)}) copy-start(bf16[512]{0:T(512)(128)(2,1)} %param.17) | copy-start | bytes 3076
  261.9 2.2 copy-start.1
  322.4 5.0 %copy-start.5 = (bf16[512]{0:T(512)(128)(2,1)S(1)}, bf16[512]{0:T(512)(128)(2,1)}, u32[]{:S(2)}) copy-start(bf16[512]{0:T(512)(128)(2,1)} %param.18) | copy-start | bytes 3076
  322.4 97.0 %all-to-all-start = ((bf16[8,512,512]{2,1,0:T(8,128)(2,1)}), bf16[8,512,512]{2,1,0:T(8,128)(2,1)}, u32[]{:S(2)}, u32[]{:S(2)}) async-start(bf16[8,512,512]{2,1,0:T(8,128)(2,1)} %bitcast.83), calls=%async_computation | async-start | bytes 8388608 | tf_op jit(solution)/shard_map/all_to_all | solution.py:33
  327.4 94.9 %copy-start = (bf16[512,512]{1,0:T(8,128)(2,1)S(1)}, bf16[512,512]{1,0:T(8,128)(2,1)}, u32[]{:S(2)}) copy-start(bf16[512,512]{1,0:T(8,128)(2,1)} %fusion.14) | copy-start | bytes 1572868
  327.4 94.9 %copy-start.2 = (bf16[2,512,512]{2,1,0:T(8,128)(2,1)S(1)}, bf16[2,512,512]{2,1,0:T(8,128)(2,1)}, u32[]{:S(2)}) copy-start(bf16[2,512,512]{2,1,0:T(8,128)(2,1)} %all-gather.8.cloned.1.call-done) | copy-start | bytes 3145732
  439.6 15.0 %copy-start.3 = (f32[64,256]{1,0:T(8,128)S(1)}, f32[64,256]{1,0:T(8,128)}, u32[]{:S(2)}) copy-start(f32[64,256]{1,0:T(8,128)} %param.25) | copy-start | bytes 196612
Sparse Core Ops, SparseCore 0:
  10.0 53.6 all-gather.7
  66.0 115.0 all-gather.9
  183.6 67.4 all-gather.11
  253.4 62.0 all-gather.13
  317.9 95.5 all-gather.15
where the time goes:
time: 462 us
  waiting for transfers between devices  291 us (63%)
  blocking collectives  107 us (23%)
  matrix products  21.6 us (5%)
  other arithmetic  18.2 us (4%)
  between operations  14 us (3%)
  starting transfers between devices  5.12 us (1%)
  local copies, waits for them, and re-layouts  5.11 us (1%)
    all_to_all x1, waiting for transfers between devices, summed_on_arrival(): lax.all_to_all(pieces, axis, split_axis=0, concat_axis=0, tiled=True)  92 us
    all_gather x1, waiting for transfers between devices, in_one_piece(): lax.all_gather(both, axis, axis=dim, tiled=True)  67 us
    all_to_all x2, blocking collectives, summed_on_arrival(): lax.all_to_all(pieces, axis, split_axis=0, concat_axis=0, tiled=True)  64.2 us
    all_gather x1, waiting for transfers between devices, on_device(): clean_all = lax.all_gather(resid_clean, 'patch', axis=1, tiled=True)  55.1 us
    all_gather x1, waiting for transfers between devices, on_device(): lax.all_gather(w_out, 'patch', axis=1, tiled=True)  48.2 us
    all_gather x1, waiting for transfers between devices, on_device(): lax.all_gather(layer_in, 'tp', axis=1, tiled=True)  27.4 us
    all_gather x1, blocking collectives, on_device(): lax.all_gather(norm_gain, 'tp', axis=0, tiled=True)  25.7 us
    psum x1, blocking collectives, on_device(): squares = lax.psum(jnp.sum(residual * residual, axis=1), 'tp')  16.9 us
  transfers between devices with their start and end apart: 6, of which 5 were waited for; matrix products, arithmetic and copies ran while one was open for 8% of the time, Pallas kernels for 0%

commit v1 on v0

v1 whole, which is shorter than its diff:
```python
import jax
import jax.numpy as jnp
from jax import lax
from jax.experimental import pallas as pl
from jax.experimental.pallas import tpu as pltpu
from jax.sharding import PartitionSpec as P

D = 4096
HD = 128
SEQ = 128
PROMPTS = 4
TOKENS = PROMPTS * SEQ
SCORED = 256
NP = 32
NT = 8
FB = D // NT
ROWS = TOKENS // NP
QCOLS = 512
KVCOL = 128
WCOLS = QCOLS + 2 * KVCOL
EPSILON = 1e-05
THETA = 500000.0
MESH = pl.DeviceIdType.MESH
F32 = jnp.float32
BF16 = jnp.bfloat16
N_SENDS = 31


class PatchGather:
    def __init__(self, own, buf, send, recv):
        self.own, self.buf, self.send, self.recv = own, buf, send, recv
        me = lax.axis_index("patch")
        self.me = me
        self.x, self.z, self.c = me // 8, (me // 2) % 4, me % 2
        self.started = []

    def block(self, dx, dz, other=False):
        c = 1 - self.c if other else self.c
        return ((self.x + dx) % 4) * 8 + ((self.z + dz) % 4) * 2 + c

    def copy(self, src, index, target, slot):
        return pltpu.make_async_remote_copy(
            src_ref=src,
            dst_ref=self.buf.at[index],
            send_sem=self.send.at[slot],
            recv_sem=self.recv.at[index],
            device_id={"patch": target},
            device_id_type=MESH,
        )

    def start(self, src, index, target):
        c = self.copy(src, index, target, len(self.started))
        c.start()
        self.started.append(c)

    def wait(self, index):
        self.copy(self.buf.at[index], index, self.block(1, 0), 0).wait_recv()

    def z_send(self):
        for dz in (1, 3, 2):
            self.start(self.own, self.me, self.block(0, dz))

    def own_send(self):
        for target in (self.block(1, 0), self.block(3, 0), self.block(0, 0, True)):
            self.start(self.own, self.me, target)

    def z_forward(self, then=None):
        for dz in (3, 1, 2):
            b = self.block(0, dz)
            self.wait(b)
            for target in (self.block(1, 0), self.block(3, 0), self.block(0, 0, True)):
                self.start(self.buf.at[b], b, target)
            if then is not None:
                then(b)

    def x_forward(self, then=None):
        for dz in (0, 3, 1, 2):
            b = self.block(3, dz)
            self.wait(b)
            if dz in (0, 3):
                self.start(self.buf.at[b], b, self.block(1, 0))
            self.start(self.buf.at[b], b, self.block(0, 0, True))
            if then is not None:
                then(b)
            b = self.block(1, dz)
            self.wait(b)
            if dz in (1, 2):
                self.start(self.buf.at[b], b, self.block(3, 0))
            self.start(self.buf.at[b], b, self.block(0, 0, True))
            if then is not None:
                then(b)

    def far(self, then=None):
        for dz in (0, 3, 1, 2):
            b = self.block(2, dz)
            self.wait(b)
            self.start(self.buf.at[b], b, self.block(0, 0, True))
            if then is not None:
                then(b)

    def core_wait(self, then=None):
        for dx, dz in [(0, 0), (0, 3), (0, 1), (0, 2)] + [
            (dx, dz) for dz in (0, 3, 1, 2) for dx in (3, 1)
        ] + [(2, dz) for dz in (0, 3, 1, 2)]:
            b = self.block(dx, dz, True)
            self.wait(b)
            if then is not None:
                then(b)

    def drain(self):
        for c in self.started:
            c.wait_send()


def greet(targets):
    barrier = pltpu.get_barrier_semaphore()
    for target in targets:
        pl.semaphore_signal(barrier, inc=1, device_id=target, device_id_type=MESH)
    pl.semaphore_wait(barrier, len(targets))


def layer_kernel(
    xin, w_ref, wo_ref, clean_ref, corrupt_ref, early_ref, late_ref, cos_ref, sin_ref, gain_ref,
    fin_ref, ssq_ref,
    xrecv, nbuf, wbuf, acc, qown, qbuf, obuf, cbuf, att, part, got,
    x_send, x_recv, w_send, w_recv, q_send, q_recv, o_send, o_recv, c_send, c_recv, r_send, r_recv,
):
    t = lax.axis_index("tp")
    w = PatchGather(w_ref, wbuf, w_send, w_recv)
    q = PatchGather(qown, qbuf, q_send, q_recv)
    o = PatchGather(wo_ref, obuf, o_send, o_recv)
    cl = PatchGather(clean_ref, cbuf, c_send, c_recv)
    me = w.me
    others = [(t + k) % NT for k in range(1, NT)]
    greet(
        [{"tp": k} for k in others]
        + [{"patch": w.block(0, dz)} for dz in (1, 3, 2)]
        + [{"patch": b} for b in (w.block(1, 0), w.block(3, 0), w.block(0, 0, True))]
    )

    def x_copy(k, target):
        return pltpu.make_async_remote_copy(
            src_ref=xin, dst_ref=xrecv.at[t], send_sem=x_send.at[k], recv_sem=x_recv.at[t],
            device_id={"tp": target}, device_id_type=MESH,
        )

    x_copies = [x_copy(k, target) for k, target in enumerate(others)]
    for c in x_copies:
        c.start()
    w.z_send()
    w.own_send()
    o.z_send()
    cl.z_send()
    obuf[me] = wo_ref[...]
    cbuf[me] = clean_ref[...]
    xrecv[t] = xin[...]

    for target in others:
        pltpu.make_async_remote_copy(
            src_ref=xin, dst_ref=xrecv.at[target], send_sem=x_send.at[0], recv_sem=x_recv.at[target],
            device_id={"tp": target}, device_id_type=MESH,
        ).wait_recv()
    total = jnp.zeros((2 * ROWS, 1), F32)
    for k in range(NT):
        v = xrecv[k, : 2 * ROWS, :].astype(F32)
        total = total + jnp.sum(v * v, axis=1, keepdims=True)
    scale = lax.rsqrt(total / D + EPSILON)
    for k in range(NT):
        v = xrecv[k, : 2 * ROWS, :].astype(F32)
        g = xrecv[k, 2 * ROWS :, :].astype(F32)[:1]
        v = (v * scale * g).astype(BF16)
        for j in range(4):
            nbuf[4 * k + j] = v[:, 128 * j : 128 * (j + 1)]

    acc[...] = jnp.dot(nbuf[me], w_ref[...], preferred_element_type=F32)

    def add(b):
        acc[...] += jnp.dot(nbuf[b], wbuf[b], preferred_element_type=F32)

    w.z_forward(add)
    w.x_forward(add)
    o.own_send()
    o.z_forward()
    w.far(add)
    w.core_wait(add)

    cosine, sine = cos_ref[...], sin_ref[...]
    for h in range(WCOLS // HD):
        v = acc[:, HD * h : HD * (h + 1)]
        if h < 5:
            v = v * cosine + pltpu.roll(v, HD // 2, 1) * sine
        v = v.astype(BF16)
        for s in range(2):
            qown[s, :, HD * h : HD * (h + 1)] = v[ROWS * s : ROWS * (s + 1)]
    q.z_send()
    q.own_send()
    qbuf[me] = qown[...]
    q.z_forward()
    q.x_forward()
    q.far()
    cl.own_send()
    cl.z_forward()
    o.x_forward()
    o.far()
    q.core_wait()
    o.core_wait()

    early = early_ref[...] > 0.5
    row = lax.broadcasted_iota(jnp.int32, (4 * SEQ, SEQ), 0) % SEQ
    col = lax.broadcasted_iota(jnp.int32, (4 * SEQ, SEQ), 1)
    causal = row >= col

    def r_copy(k, n, target):
        rows = pl.ds(SEQ * n, SEQ)
        return pltpu.make_async_remote_copy(
            src_ref=part.at[target, rows], dst_ref=got.at[t, rows],
            send_sem=r_send.at[k, n], recv_sem=r_recv.at[t, n],
            device_id={"tp": target}, device_id_type=MESH,
        )

    r_copies = []
    for n in range(PROMPTS):
        def picked(lo, hi, n=n):
            a = qbuf[8 * n : 8 * (n + 1), 0, :, lo:hi].reshape(SEQ, hi - lo).astype(F32)
            b = qbuf[8 * n : 8 * (n + 1), 1, :, lo:hi].reshape(SEQ, hi - lo).astype(F32)
            return jnp.where(early, b, a).astype(BF16)

        queries = jnp.concatenate([picked(HD * h, HD * (h + 1)) for h in range(4)], axis=0)
        keys = picked(QCOLS, QCOLS + HD)
        values = picked(QCOLS + HD, QCOLS + 2 * HD)
        scores = lax.dot_general(
            queries, keys, (((1,), (1,)), ((), ())), preferred_element_type=F32
        ) * HD ** (-0.5)
        scores = jnp.where(causal, scores, -1e30)
        scores = jnp.exp(scores - jnp.max(scores, axis=1, keepdims=True))
        probs = (scores / jnp.sum(scores, axis=1, keepdims=True)).astype(BF16)
        heads = jnp.dot(probs, values, preferred_element_type=F32).astype(BF16)
        for h in range(4):
            att[:, HD * h : HD * (h + 1)] = heads[SEQ * h : SEQ * (h + 1)]
        rows = pl.ds(SEQ * n, SEQ)
        for k, target in enumerate(others + [t]):
            for j in range(2):
                b = 4 * target + 2 * j
                both = jnp.concatenate([obuf[b], obuf[b + 1]], axis=1)
                piece = jnp.dot(att[...], both, preferred_element_type=F32)
                part[target, rows, 256 * j : 256 * (j + 1)] = piece.astype(BF16)
            if k < NT - 1:
                c = r_copy(k, n, target)
                c.start()
                r_copies.append(c)

    cl.x_forward()
    cl.far()
    cl.core_wait()

    gain = gain_ref[...].astype(F32)
    for n in range(PROMPTS):
        rows = pl.ds(SEQ * n, SEQ)
        for target in others:
            pltpu.make_async_remote_copy(
                src_ref=part.at[target, rows], dst_ref=got.at[target, rows],
                send_sem=r_send.at[0, n], recv_sem=r_recv.at[target, n],
                device_id={"tp": target}, device_id_type=MESH,
            ).wait_recv()

        def finish(i, carry, n=n):
            at = pl.ds(pl.multiple_of(SEQ * n + ROWS * i, ROWS), ROWS)
            local = pl.ds(pl.multiple_of(ROWS * i, ROWS), ROWS)
            e = early_ref[local, :1] > 0.5
            late = late_ref[local, :1] > 0.5
            v = corrupt_ref[at, :].astype(F32)
            v = jnp.where(e, cbuf[8 * n + i, 0].astype(F32), v)
            head = part[t, at, :].astype(F32)
            for target in others:
                head = head + got[target, at, :].astype(F32)
            v = v + head
            v = jnp.where(late, cbuf[8 * n + i, 1].astype(F32), v)
            ssq_ref[at, :] = jnp.broadcast_to(jnp.sum(v * v, axis=1, keepdims=True), (ROWS, 128))
            fin_ref[at, :] = (v * gain).astype(BF16)
            return carry

        lax.fori_loop(0, SEQ // ROWS, finish, 0)

    for c in x_copies + r_copies:
        c.wait_send()
    for g in (w, q, o, cl):
        g.drain()


def layer(xin, wqkv, wout, clean, corrupt, early, late, cosine, sine, gain):
    vmem = pl.BlockSpec(memory_space=pltpu.VMEM)
    dma = pltpu.SemaphoreType.DMA
    return pl.pallas_call(
        layer_kernel,
        out_shape=(
            jax.ShapeDtypeStruct((TOKENS, FB), BF16),
            jax.ShapeDtypeStruct((TOKENS, 128), F32),
        ),
        in_specs=[vmem] * 10,
        out_specs=(vmem, vmem),
        scratch_shapes=[
            pltpu.VMEM((NT, 3 * ROWS, FB), BF16),
            pltpu.VMEM((NP, 2 * ROWS, 128), BF16),
            pltpu.VMEM((NP, 128, WCOLS), BF16),
            pltpu.VMEM((2 * ROWS, WCOLS), F32),
            pltpu.VMEM((2, ROWS, WCOLS), BF16),
            pltpu.VMEM((NP, 2, ROWS, WCOLS), BF16),
            pltpu.VMEM((NP, FB, 128), BF16),
            pltpu.VMEM((NP, 2, ROWS, FB), BF16),
            pltpu.VMEM((SEQ, FB), BF16),
            pltpu.VMEM((NT, TOKENS, FB), BF16),
            pltpu.VMEM((NT, TOKENS, FB), BF16),
            dma((NT,)), dma((NT,)),
            dma((N_SENDS,)), dma((NP,)),
            dma((N_SENDS,)), dma((NP,)),
            dma((N_SENDS,)), dma((NP,)),
            dma((N_SENDS,)), dma((NP,)),
            dma((NT, PROMPTS)), dma((NT, PROMPTS)),
        ],
        compiler_params=pltpu.CompilerParams(
            collective_id=0, has_side_effects=True, vmem_limit_bytes=56 * 1024 * 1024
        ),
        cost_estimate=pl.CostEstimate(
            flops=4 * 10**9, bytes_accessed=20 * 2**20, transcendentals=10**6
        ),
        name="layer",
    )(xin, wqkv, wout, clean, corrupt, early, late, cosine, sine, gain)


def logits_kernel(fin_ref, ssq_ref, score_ref, base_ref, out_ref, lg, lgot, sgot, l_send, l_recv, s_send, s_recv):
    t = lax.axis_index("tp")
    others = [(t + k) % NT for k in range(1, NT)]
    greet([{"tp": k} for k in others])
    part = TOKENS // NT

    def s_copy(k, target, to):
        return pltpu.make_async_remote_copy(
            src_ref=ssq_ref.at[pl.ds(pl.multiple_of(part * target, part), part)], dst_ref=sgot.at[to],
            send_sem=s_send.at[k], recv_sem=s_recv.at[to],
            device_id={"tp": target}, device_id_type=MESH,
        )

    def l_copy(k, target, to):
        return pltpu.make_async_remote_copy(
            src_ref=lg.at[target], dst_ref=lgot.at[to],
            send_sem=l_send.at[k], recv_sem=l_recv.at[to],
            device_id={"tp": target}, device_id_type=MESH,
        )

    copies = []
    for k, target in enumerate(others):
        copies.append(s_copy(k, target, t))
        copies[-1].start()
    value = lax.dot_general(
        fin_ref[...], score_ref[...], (((1,), (1,)), ((), ())), preferred_element_type=F32
    ).astype(BF16)
    lg[...] = value.reshape(NT, part, SCORED)
    for k, target in enumerate(others):
        copies.append(l_copy(k, target, t))
        copies[-1].start()
    logits = lg[t].astype(F32)
    total = ssq_ref[pl.ds(pl.multiple_of(part * t, part), part), :]
    for target in others:
        s_copy(0, target, target).wait_recv()
        l_copy(0, target, target).wait_recv()
        logits = logits + lgot[target].astype(F32)
        total = total + sgot[target]
    scale = lax.rsqrt(total / D + EPSILON)
    out_ref[...] = logits * scale[:, :1] - base_ref[...]
    for c in copies:
        c.wait_send()


def logits_call(fin, ssq, score, base):
    vmem = pl.BlockSpec(memory_space=pltpu.VMEM)
    dma = pltpu.SemaphoreType.DMA
    part = TOKENS // NT
    return pl.pallas_call(
        logits_kernel,
        out_shape=jax.ShapeDtypeStruct((part, SCORED), F32),
        in_specs=[vmem] * 4,
        out_specs=vmem,
        scratch_shapes=[
            pltpu.VMEM((NT, part, SCORED), BF16),
            pltpu.VMEM((NT, part, SCORED), BF16),
            pltpu.VMEM((NT, part, 128), F32),
            dma((NT,)), dma((NT,)), dma((NT,)), dma((NT,)),
        ],
        compiler_params=pltpu.CompilerParams(collective_id=1, has_side_effects=True),
        cost_estimate=pl.CostEstimate(
            flops=2 * 10**8, bytes_accessed=2**21, transcendentals=1000
        ),
        name="logits",
    )(fin, ssq, score, base)


def rope_rows(first):
    half = HD // 2
    freqs = THETA ** (-(jnp.arange(half, dtype=F32) * 2.0 / HD))
    angles = (first + jnp.arange(ROWS)).astype(F32)[:, None] * freqs[None, :]
    cosine, sine = jnp.cos(angles), jnp.sin(angles)
    return (
        jnp.tile(jnp.concatenate([cosine, cosine], axis=1), (2, 1)),
        jnp.tile(jnp.concatenate([-sine, sine], axis=1), (2, 1)),
    )


def on_device(
    resid_corrupt, resid_clean, patch_level, patch_mask, norm_gain, final_gain,
    w_query, w_key, w_value, w_out, unembed, scored_ids, base_logits,
):
    p = lax.axis_index("patch")
    t = lax.axis_index("tp")
    rows_dev = unembed.shape[0]
    first_row = (p * NT + t) * rows_dev
    owned_rows = (scored_ids[:, None] == first_row + lax.iota(jnp.int32, rows_dev)[None, :]).astype(BF16)
    chosen = jnp.dot(owned_rows, unembed, preferred_element_type=F32).astype(BF16)
    score_all = lax.psum(chosen, ("patch", "tp"))

    level = patch_level[0]
    spliced = patch_mask[0][:, None] == 1
    early = jnp.broadcast_to((spliced & (level == 0)).astype(F32), (SEQ, 128))
    late = jnp.broadcast_to((spliced & (level == 1)).astype(F32), (SEQ, 128))
    xin = jnp.concatenate(
        [
            lax.dynamic_slice_in_dim(resid_corrupt, p * ROWS, ROWS, axis=0),
            resid_clean[0],
            jnp.broadcast_to(norm_gain[None, :], (ROWS, FB)),
        ],
        axis=0,
    )
    wqkv = jnp.concatenate([w_query, w_key, w_value], axis=1)
    cosine, sine = rope_rows((p * ROWS) % SEQ)
    fin, ssq = layer(
        xin, wqkv, w_out, resid_clean, resid_corrupt, early, late, cosine, sine, final_gain[None, :]
    )
    score = lax.dynamic_slice_in_dim(score_all, t * FB, FB, axis=1)
    return logits_call(fin, ssq, score, base_logits)[None]


def solution(mesh):
    placed = (
        P(None, "tp"),
        P(None, "patch", "tp"),
        P("patch"),
        P("patch", None),
        P("tp"),
        P("tp"),
        P("patch", "tp"),
        P("patch", "tp"),
        P("patch", "tp"),
        P("tp", "patch"),
        P(("patch", "tp"), None),
        P(),
        P("tp", None),
    )
    return jax.shard_map(
        on_device, mesh=mesh, in_specs=placed, out_specs=P("patch", "tp", None), check_vma=False
    )
```

time: 462 us -> 318 us (0.69)
  waiting for transfers between devices: 291 us -> 139 us
  Pallas kernels: 0 us -> 151 us
  blocking collectives: 107 us -> 0 us
  matrix products: 21.6 us -> 4.93 us
  other arithmetic: 18.2 us -> 1.53 us
  starting transfers between devices: 5.12 us -> 0.01 us
    all_gather x5 -> x0, waiting for transfers between devices: 198 us -> none  [the longest x1 67 us: in_one_piece(): lax.all_gather(both, axis, axis=dim, tiled=True)]
    pallas_call x0 -> x2, Pallas kernels: none -> 151 us  [the longest x1 139 us: layer(): pl.pallas_call(layer_kernel, out_shape=(jax.ShapeDtypeStruct((TOKENS, FB)...]
    psum x0 -> x1, waiting for transfers between devices: none -> 139 us  [on_device(): score_all = lax.psum(chosen, ('patch', 'tp'))]
    all_to_all x1 -> x0, waiting for transfers between devices: 92 us -> none  [summed_on_arrival(): lax.all_to_all(pieces, axis, split_axis=0, concat_axis=0, tiled=True)]
    all_to_all x2 -> x0, blocking collectives: 64.2 us -> none  [summed_on_arrival(): lax.all_to_all(pieces, axis, split_axis=0, concat_axis=0, tiled=True)]
    all_gather x1 -> x0, blocking collectives: 25.7 us -> none  [on_device(): lax.all_gather(norm_gain, 'tp', axis=0, tiled=True)]
    psum x1 -> x0, blocking collectives: 16.9 us -> none  [on_device(): squares = lax.psum(jnp.sum(residual * residual, axis=1), 'tp')]
    dot_general x8 -> x1, matrix products: 21.6 us -> 4.93 us  [on_device(): jnp.dot(owned_rows, unembed, preferred_element_type=F32).astype(BF16)]
  transfers between devices with their start and end apart: 6 -> 1, of which waited for: 5 -> 1; matrix products, arithmetic and copies ran while one was open for 8% -> 2% of each run, Pallas kernels for 0% -> 44%
where the time goes in v1:
time: 318 us; the launch traced here: 317 us
  Pallas kernels  151 us (47%)
  waiting for transfers between devices  139 us (44%)
  between operations  14.2 us (4%)
  local copies, waits for them, and re-layouts  7.09 us (2%)
  matrix products  4.93 us (2%)
    pallas_call x1, Pallas kernels, layer(): pl.pallas_call(layer_kernel, out_shape=(jax.ShapeDtypeStruct((TOKENS, FB)...  139 us
    psum x1, waiting for transfers between devices, on_device(): score_all = lax.psum(chosen, ('patch', 'tp'))  139 us
    pallas_call x1, Pallas kernels, logits_call(): pl.pallas_call(logits_kernel, out_shape=jax.ShapeDtypeStruct((part, SCORE...  11.1 us
  transfers between devices with their start and end apart: 1, of which 1 were waited for; matrix products, arithmetic and copies ran while one was open for 2% of the time, Pallas kernels for 44%

profile of v1, /device:TPU:2, one launch (start us, length us, event | category | flops | bytes accessed | tf_op | source)
XLA Modules:
  0.0 317.0 jit_solution(10515194203876653452)
XLA Ops:
  6.5 0.0 all-reduce.2.cloned.1.call-start
  6.5 0.0 copy-start.4
  6.5 0.0 copy-start.3
  6.5 0.0 copy-start.5
  6.6 0.0 copy-start
  6.6 0.0 copy-start.1
  6.6 0.0 copy-start.2
  6.6 0.0 copy-start.6
  6.6 4.9 %convolution_convert_fusion = bf16[256,4096]{1,0:T(8,128)(2,1)} fusion(bf16[501,4096]{1,0:T(8,128)(2,1)} %param.23, s32[501]{0:T(512)S(1)} %iota_add_fusion, s32[256]{0:T(256)} %param.24), kind=kOutput, calls=%fused_computation | convolution fusion | flops 1051849984 | bytes 6204372 | tf_op jit(solution)/shard_map/dot_general | solution.py:417
  11.5 0.0 all-reduce.2.cloned.1.call-update
  12.3 0.0 copy-done.4
  12.3 0.6 broadcast_in_dim.13.gain_ref
  12.9 0.7 constant_dynamic-slice_fusion.1
  13.6 0.1 fusion.3
  13.7 0.1 pad_maximum_fusion.2
  13.8 0.0 copy-done.3
  13.8 0.0 copy-done.5
  13.8 0.6 pad_maximum_fusion.1.xin
  14.4 0.0 copy-done
  14.4 0.0 copy-done.1
  14.4 0.0 copy-done.2
  14.4 0.7 pad_maximum_fusion.w_ref
  15.1 0.0 copy-done.6
  15.1 0.6 tile.8
  15.7 0.6 tile.20
  16.3 0.7 broadcast_in_dim.12.late_ref
  17.0 0.7 broadcast_in_dim.11.early_ref
  17.7 139.4 %layer.1 = (bf16[512,512]{1,0:T(8,128)(2,1)}, f32[512,128]{1,0:T(8,128)}) custom-call(bf16[48,512]{1,0:T(8,128)(2,1)} %pad_maximum_fusion.1.xin, bf16[128,768]{1,0:T(8,128)(2,1)} %pad_maximum_fusion.w_ref, bf16[512,128]{1,0:T(8,128)(2,1)} %wo_ref.1, bf16[2,16,512]{2,1,0:T(8,128)(2,1)} %clean_ref.1, bf16[512,512]{1,0:T(8,128)(2,1)} %corrupt_ref.1, ...), custom_call_target="tpu_custom_call" | custom-call | flops 4000000000 | bytes 20971520 | tf_op jit(solution)/shard_map/layer/pallas_call | solution.py:293
  157.2 138.8 %all-reduce.2.cloned.1.call-done = bf16[256,4096]{1,0:T(8,128)(2,1)} async-done(((bf16[256,4096]{1,0:T(8,128)(2,1)}), bf16[256,4096]{1,0:T(8,128)(2,1)}) %all-reduce.2.cloned.1.call-update) | async-done | bytes 2097168 | tf_op jit(solution)/shard_map/psum | solution.py:418
  295.9 1.7 constant_dynamic-slice_fusion.score_ref
  297.6 11.1 %logits.1 = f32[64,256]{1,0:T(8,128)} custom-call(bf16[512,512]{1,0:T(8,128)(2,1)} %get-tuple-element.7.fin_ref, f32[512,128]{1,0:T(8,128)} %get-tuple-element.8.ssq_ref, bf16[256,512]{1,0:T(8,128)(2,1)} %constant_dynamic-slice_fusion.score_ref, f32[64,256]{1,0:T(8,128)} %base_ref.1), custom_call_target="tpu_custom_call" | custom-call | flops 200000000 | bytes 2097152 | tf_op jit(solution)/shard_map/logits/pallas_call | solution.py:378
  308.7 1.5 copy.17
  (6 shorter events, 0.0 us)
Async XLA Ops:
  6.5 289.4 %all-reduce.2.cloned.1.call-start = ((), (), s32[]{:S(2)}) async-start(), calls=%async_computation | async-start | bytes 4194304 | tf_op jit(solution)/shard_map/psum | solution.py:418
  6.5 5.7 %copy-start.4 = (bf16[512]{0:T(512)(128)(2,1)S(1)}, bf16[512]{0:T(512)(128)(2,1)}, u32[]{:S(2)}) copy-start(bf16[512]{0:T(512)(128)(2,1)} %param.18) | copy-start | bytes 3076
  6.5 7.2 %copy-start.3 = (bf16[2,16,512]{2,1,0:T(8,128)(2,1)S(1)}, bf16[2,16,512]{2,1,0:T(8,128)(2,1)}, u32[]{:S(2)}) copy-start(bf16[2,16,512]{2,1,0:T(8,128)(2,1)} %clean_ref.1) | copy-start | bytes 98308
  6.5 7.2 %copy-start.5 = (bf16[512]{0:T(512)(128)(2,1)S(1)}, bf16[512]{0:T(512)(128)(2,1)}, u32[]{:S(2)}) copy-start(bf16[512]{0:T(512)(128)(2,1)} %param.17) | copy-start | bytes 3076
  6.6 7.9 %copy-start = (bf16[128,512]{1,0:T(8,128)(2,1)S(1)}, bf16[128,512]{1,0:T(8,128)(2,1)}, u32[]{:S(2)}) copy-start(bf16[128,512]{1,0:T(8,128)(2,1)} %param.19) | copy-start | bytes 393220
  6.6 7.9 %copy-start.1 = (bf16[128,128]{1,0:T(8,128)(2,1)S(1)}, bf16[128,128]{1,0:T(8,128)(2,1)}, u32[]{:S(2)}) copy-start(bf16[128,128]{1,0:T(8,128)(2,1)} %param.21) | copy-start | bytes 98308
  6.6 7.8 %copy-start.2 = (bf16[128,128]{1,0:T(8,128)(2,1)S(1)}, bf16[128,128]{1,0:T(8,128)(2,1)}, u32[]{:S(2)}) copy-start(bf16[128,128]{1,0:T(8,128)(2,1)} %param.20) | copy-start | bytes 98308
  6.6 8.5 %copy-start.6 = (s32[1,128]{1,0:T(1,128)S(1)}, s32[1,128]{1,0:T(1,128)}, u32[]{:S(2)}) copy-start(s32[1,128]{1,0:T(1,128)} %param.16) | copy-start | bytes 1540
Sparse Core Ops, SparseCore 0:
  12.7 283.1 all-reduce.1

commit v2 on v1

v2 whole, which is shorter than its diff:
```python
import jax
import jax.numpy as jnp
import numpy as np
from jax import lax
from jax.experimental import pallas as pl
from jax.experimental.pallas import tpu as pltpu
from jax.sharding import PartitionSpec as P

D = 4096
HD = 128
SEQ = 128
PROMPTS = 4
TOKENS = PROMPTS * SEQ
SCORED = 256
NP = 32
NT = 8
FB = D // NT
ROWS = TOKENS // NP
QCOLS = 512
KVCOL = 128
WCOLS = QCOLS + 2 * KVCOL
EPSILON = 1e-05
THETA = 500000.0
MESH = pl.DeviceIdType.MESH
F32 = jnp.float32
BF16 = jnp.bfloat16
N_SENDS = 31


class PatchGather:
    def __init__(self, own, buf, send, recv):
        self.own, self.buf, self.send, self.recv = own, buf, send, recv
        me = lax.axis_index("patch")
        self.me = me
        self.x, self.z, self.c = me // 8, (me // 2) % 4, me % 2
        self.started = []

    def block(self, dx, dz, other=False):
        c = 1 - self.c if other else self.c
        return ((self.x + dx) % 4) * 8 + ((self.z + dz) % 4) * 2 + c

    def copy(self, src, index, target, slot):
        return pltpu.make_async_remote_copy(
            src_ref=src,
            dst_ref=self.buf.at[index],
            send_sem=self.send.at[slot],
            recv_sem=self.recv.at[index],
            device_id={"patch": target},
            device_id_type=MESH,
        )

    def start(self, src, index, target):
        c = self.copy(src, index, target, len(self.started))
        c.start()
        self.started.append(c)

    def wait(self, index):
        self.copy(self.buf.at[index], index, self.block(1, 0), 0).wait_recv()

    def z_send(self):
        for dz in (1, 3, 2):
            self.start(self.own, self.me, self.block(0, dz))

    def own_send(self):
        for target in (self.block(1, 0), self.block(3, 0), self.block(0, 0, True)):
            self.start(self.own, self.me, target)

    def z_forward(self, then=None):
        for dz in (3, 1, 2):
            b = self.block(0, dz)
            self.wait(b)
            for target in (self.block(1, 0), self.block(3, 0), self.block(0, 0, True)):
                self.start(self.buf.at[b], b, target)
            if then is not None:
                then(b)

    def x_forward(self, then=None):
        for dz in (0, 3, 1, 2):
            b = self.block(3, dz)
            self.wait(b)
            if dz in (0, 3):
                self.start(self.buf.at[b], b, self.block(1, 0))
            self.start(self.buf.at[b], b, self.block(0, 0, True))
            if then is not None:
                then(b)
            b = self.block(1, dz)
            self.wait(b)
            if dz in (1, 2):
                self.start(self.buf.at[b], b, self.block(3, 0))
            self.start(self.buf.at[b], b, self.block(0, 0, True))
            if then is not None:
                then(b)

    def far(self, then=None):
        for dz in (0, 3, 1, 2):
            b = self.block(2, dz)
            self.wait(b)
            self.start(self.buf.at[b], b, self.block(0, 0, True))
            if then is not None:
                then(b)

    def core_wait(self, then=None):
        for dx, dz in [(0, 0), (0, 3), (0, 1), (0, 2)] + [
            (dx, dz) for dz in (0, 3, 1, 2) for dx in (3, 1)
        ] + [(2, dz) for dz in (0, 3, 1, 2)]:
            b = self.block(dx, dz, True)
            self.wait(b)
            if then is not None:
                then(b)

    def drain(self):
        for c in self.started:
            c.wait_send()


def greet(targets):
    barrier = pltpu.get_barrier_semaphore()
    for target in targets:
        pl.semaphore_signal(barrier, inc=1, device_id=target, device_id_type=MESH)
    pl.semaphore_wait(barrier, len(targets))


def layer_kernel(
    corrupt_hbm, clean_hbm, wq_hbm, wk_hbm, wv_hbm, wo_hbm, unembed_hbm,
    level_ref, mask_ref, ids_ref, ngain_ref, fgain_ref, cos_ref, sin_ref, base_ref,
    out_ref,
    corrupt_ref, clean_ref, w_ref, wo_ref, unembed_ref,
    xin, xrecv, nbuf, wbuf, acc, qown, qbuf, obuf, cbuf, att, part, got, early_ref, late_ref,
    chosen, chosen_got, paired, spread, spread_z, sum_z, sum_x, own_x, score, fin, ssq, ssq_got, lg, lg_got,
    local, x_send, x_recv, w_send, w_recv, q_send, q_recv, o_send, o_recv, c_send, c_recv, r_send, r_recv,
    s_send, s_recv, sz_recv, sx_recv, sg_recv, l_send, l_recv, n_send, n_recv,
):
    t = lax.axis_index("tp")
    w = PatchGather(w_ref, wbuf, w_send, w_recv)
    q = PatchGather(qown, qbuf, q_send, q_recv)
    o = PatchGather(wo_ref, obuf, o_send, o_recv)
    cl = PatchGather(clean_ref, cbuf, c_send, c_recv)
    me, px, pz, pc = w.me, w.x, w.z, w.c
    others = [(t + k) % NT for k in range(1, NT)]
    z_others = [(k, (pz + k) % 4) for k in (1, 3, 2)]
    x_others = [(k, (px + k) % 4) for k in (1, 3, 2)]
    partner = w.block(0, 0, True)

    loads = [
        pltpu.make_async_copy(src, dst, local.at[k])
        for k, (src, dst) in enumerate(
            [
                (wq_hbm, w_ref.at[:, pl.ds(0, QCOLS)]),
                (wk_hbm, w_ref.at[:, pl.ds(QCOLS, KVCOL)]),
                (wv_hbm, w_ref.at[:, pl.ds(QCOLS + KVCOL, KVCOL)]),
                (clean_hbm, clean_ref),
                (wo_hbm, wo_ref),
                (corrupt_hbm, corrupt_ref),
                (unembed_hbm, unembed_ref),
            ]
        )
    ]
    for c in loads:
        c.start()
    for c in loads[:6]:
        c.wait()
    xin[:ROWS] = corrupt_ref[pl.ds(pl.multiple_of(me * ROWS, ROWS), ROWS), :]
    xin[ROWS : 2 * ROWS] = clean_ref[0]
    xin[2 * ROWS :] = jnp.broadcast_to(ngain_ref[...].astype(F32), (ROWS, FB)).astype(BF16)
    spliced = jnp.transpose(jnp.broadcast_to(mask_ref[...].astype(F32), (SEQ, SEQ)))
    level = level_ref[0].astype(F32)
    early_ref[...] = spliced * (1.0 - level)
    late_ref[...] = spliced * level
    obuf[me] = wo_ref[...]
    cbuf[me] = clean_ref[...]
    xrecv[t] = xin[...]
    greet(
        [{"tp": k} for k in others]
        + [{"patch": w.block(0, dz)} for dz in (1, 3, 2)]
        + [{"patch": w.block(dx, 0)} for dx in (1, 3, 2)]
        + [{"patch": partner}]
    )

    def x_copy(k, target):
        return pltpu.make_async_remote_copy(
            src_ref=xin, dst_ref=xrecv.at[t], send_sem=x_send.at[k], recv_sem=x_recv.at[t],
            device_id={"tp": target}, device_id_type=MESH,
        )

    started = [x_copy(k, target) for k, target in enumerate(others)]
    for c in started:
        c.start()
    w.z_send()
    w.own_send()
    o.z_send()
    cl.z_send()

    def s_copy(src, dst, send, recv, where):
        return pltpu.make_async_remote_copy(
            src_ref=src, dst_ref=dst, send_sem=s_send.at[send], recv_sem=recv,
            device_id=where, device_id_type=MESH,
        )

    def begin(c):
        c.start()
        started.append(c)

    loads[6].wait()
    rows_dev = unembed_ref.shape[0]
    wanted = ids_ref[...] - (me * NT + t) * rows_dev
    owned = jnp.where(
        wanted == lax.broadcasted_iota(jnp.int32, (SCORED, rows_dev), 1), 1.0, 0.0
    ).astype(BF16)
    for k in range(NT):
        chosen[k] = jnp.dot(
            owned, unembed_ref[:, FB * k : FB * (k + 1)], preferred_element_type=F32
        ).astype(BF16)
    half = SCORED // 2
    pair = s_copy(
        chosen.at[:, pl.ds(pl.multiple_of(half * (1 - pc), half), half)],
        chosen_got, 0, s_recv.at[0], {"patch": partner},
    )
    begin(pair)

    for target in others:
        pltpu.make_async_remote_copy(
            src_ref=xin, dst_ref=xrecv.at[target], send_sem=x_send.at[0], recv_sem=x_recv.at[target],
            device_id={"tp": target}, device_id_type=MESH,
        ).wait_recv()
    total = jnp.zeros((2 * ROWS, 1), F32)
    for k in range(NT):
        v = xrecv[k, : 2 * ROWS, :].astype(F32)
        total = total + jnp.sum(v * v, axis=1, keepdims=True)
    scale = lax.rsqrt(total / D + EPSILON)
    for k in range(NT):
        v = xrecv[k, : 2 * ROWS, :].astype(F32)
        g = xrecv[k, 2 * ROWS :, :].astype(F32)[:1]
        v = (v * scale * g).astype(BF16)
        for j in range(4):
            nbuf[4 * k + j] = v[:, 128 * j : 128 * (j + 1)]

    acc[...] = jnp.dot(nbuf[me], w_ref[...], preferred_element_type=F32)

    def add(b):
        acc[...] += jnp.dot(nbuf[b], wbuf[b], preferred_element_type=F32)

    w.z_forward(add)

    pair.wait_recv()
    paired[...] = chosen[:, pl.ds(pl.multiple_of(half * pc, half), half)] + chosen_got[...]
    for k, target in enumerate(others):
        begin(s_copy(paired.at[target], spread.at[t], 1 + k, s_recv.at[1 + t], {"tp": target}))

    w.x_forward(add)
    o.own_send()
    o.z_forward()

    v = paired[t]
    for target in others:
        s_copy(paired.at[target], spread.at[target], 0, s_recv.at[1 + target], {"tp": target}).wait_recv()
        v = v + spread[target]
    spread_z[...] = v.reshape(4, half // 4, FB)
    for k, target in z_others:
        begin(s_copy(spread_z.at[target], sum_z.at[pz], 8 + k, sz_recv.at[pz], {"patch": w.block(0, k)}))

    w.far(add)
    w.core_wait(add)

    at = pl.ds(pl.multiple_of((me * ROWS) % SEQ, ROWS), ROWS)
    cosine = jnp.concatenate([cos_ref[at, :]] * 2, axis=0)
    sine = jnp.concatenate([sin_ref[at, :]] * 2, axis=0)
    for h in range(WCOLS // HD):
        v = acc[:, HD * h : HD * (h + 1)]
        if h < 5:
            v = v * cosine + pltpu.roll(v, HD // 2, 1) * sine
        v = v.astype(BF16)
        for s in range(2):
            qown[s, :, HD * h : HD * (h + 1)] = v[ROWS * s : ROWS * (s + 1)]
    q.z_send()
    q.own_send()
    qbuf[me] = qown[...]

    v = spread_z[pz]
    for k, target in z_others:
        s_copy(spread_z.at[target], sum_z.at[target], 0, sz_recv.at[target], {"patch": w.block(0, k)}).wait_recv()
        v = v + sum_z[target]
    own_x[...] = v
    for k, target in x_others:
        begin(s_copy(own_x, sum_x.at[px], 12 + k, sx_recv.at[px], {"patch": w.block(k, 0)}))

    q.z_forward()
    q.x_forward()

    v = own_x[...]
    for k, target in x_others:
        s_copy(own_x, sum_x.at[target], 0, sx_recv.at[target], {"patch": w.block(k, 0)}).wait_recv()
        v = v + sum_x[target]
    score[pc, pz] = v
    for k, target in z_others:
        begin(s_copy(score.at[pc, pz], score.at[pc, pz], 16 + k, sg_recv.at[pz], {"patch": w.block(0, k)}))

    q.far()
    cl.own_send()
    cl.z_forward()
    o.x_forward()
    o.far()
    for k, target in z_others:
        s_copy(score.at[pc, target], score.at[pc, target], 0, sg_recv.at[target], {"patch": w.block(0, k)}).wait_recv()
    begin(s_copy(score.at[pc], score.at[pc], 20, s_recv.at[9], {"patch": partner}))
    q.core_wait()
    o.core_wait()

    early = early_ref[...] > 0.5
    row = lax.broadcasted_iota(jnp.int32, (4 * SEQ, SEQ), 0) % SEQ
    col = lax.broadcasted_iota(jnp.int32, (4 * SEQ, SEQ), 1)
    causal = row >= col

    def r_copy(k, n, target, to):
        rows = pl.ds(SEQ * n, SEQ)
        return pltpu.make_async_remote_copy(
            src_ref=part.at[target, rows], dst_ref=got.at[to, rows],
            send_sem=r_send.at[k, n], recv_sem=r_recv.at[to, n],
            device_id={"tp": target}, device_id_type=MESH,
        )

    for n in range(PROMPTS):
        def picked(lo, hi, n=n):
            a = qbuf[8 * n : 8 * (n + 1), 0, :, lo:hi].reshape(SEQ, hi - lo).astype(F32)
            b = qbuf[8 * n : 8 * (n + 1), 1, :, lo:hi].reshape(SEQ, hi - lo).astype(F32)
            return jnp.where(early, b, a).astype(BF16)

        queries = jnp.concatenate([picked(HD * h, HD * (h + 1)) for h in range(4)], axis=0)
        keys = picked(QCOLS, QCOLS + HD)
        values = picked(QCOLS + HD, QCOLS + 2 * HD)
        scores = lax.dot_general(
            queries, keys, (((1,), (1,)), ((), ())), preferred_element_type=F32
        ) * HD ** (-0.5)
        scores = jnp.where(causal, scores, -1e30)
        scores = jnp.exp(scores - jnp.max(scores, axis=1, keepdims=True))
        probs = (scores / jnp.sum(scores, axis=1, keepdims=True)).astype(BF16)
        heads = jnp.dot(probs, values, preferred_element_type=F32).astype(BF16)
        for h in range(4):
            att[:, HD * h : HD * (h + 1)] = heads[SEQ * h : SEQ * (h + 1)]
        rows = pl.ds(SEQ * n, SEQ)
        for k, target in enumerate(others + [t]):
            for j in range(2):
                b = 4 * target + 2 * j
                both = jnp.concatenate([obuf[b], obuf[b + 1]], axis=1)
                piece = jnp.dot(att[...], both, preferred_element_type=F32)
                part[target, rows, 256 * j : 256 * (j + 1)] = piece.astype(BF16)
            if k < NT - 1:
                begin(r_copy(k, n, target, t))

    cl.x_forward()
    cl.far()
    cl.core_wait()
    s_copy(score.at[pc], score.at[1 - pc], 0, s_recv.at[9], {"patch": partner}).wait_recv()

    gain = fgain_ref[...].astype(F32)
    share = TOKENS // NT

    def l_copy(target, to):
        return pltpu.make_async_remote_copy(
            src_ref=lg.at[target], dst_ref=lg_got.at[to], send_sem=l_send.at[target], recv_sem=l_recv.at[to],
            device_id={"tp": target}, device_id_type=MESH,
        )

    def n_copy(target, to):
        return pltpu.make_async_remote_copy(
            src_ref=ssq.at[target], dst_ref=ssq_got.at[to], send_sem=n_send.at[target], recv_sem=n_recv.at[to],
            device_id={"tp": target}, device_id_type=MESH,
        )

    for n in range(PROMPTS):
        for target in others:
            r_copy(0, n, target, target).wait_recv()

        def finish(i, carry, n=n):
            at = pl.ds(pl.multiple_of(SEQ * n + ROWS * i, ROWS), ROWS)
            local_at = pl.ds(pl.multiple_of(ROWS * i, ROWS), ROWS)
            e = early_ref[local_at, :1] > 0.5
            late = late_ref[local_at, :1] > 0.5
            v = corrupt_ref[at, :].astype(F32)
            v = jnp.where(e, cbuf[8 * n + i, 0].astype(F32), v)
            head = part[t, at, :].astype(F32)
            for target in others:
                head = head + got[target, at, :].astype(F32)
            v = v + head
            v = jnp.where(late, cbuf[8 * n + i, 1].astype(F32), v)
            within = pl.ds(pl.multiple_of(ROWS * (i % 4), ROWS), ROWS)
            ssq[2 * n + i // 4, within, :] = jnp.broadcast_to(
                jnp.sum(v * v, axis=1, keepdims=True), (ROWS, 128)
            )
            fin[local_at, :] = (v * gain).astype(BF16)
            return carry

        lax.fori_loop(0, SEQ // ROWS, finish, 0)
        value = lax.dot_general(
            fin[...], score[...].reshape(SCORED, FB), (((1,), (1,)), ((), ())),
            preferred_element_type=F32,
        ).astype(BF16)
        for s in range(2):
            target = 2 * n + s
            lg[target] = value[share * s : share * (s + 1)]

            @pl.when(target != t)
            def _(target=target):
                n_copy(target, t).start()
                l_copy(target, t).start()

    logits = lg[t].astype(F32)
    total = ssq[t]
    for target in others:
        n_copy(target, target).wait_recv()
        l_copy(target, target).wait_recv()
        logits = logits + lg_got[target].astype(F32)
        total = total + ssq_got[target]
    scale = lax.rsqrt(total / D + EPSILON)
    out_ref[...] = logits * scale[:, :1] - base_ref[...]

    for target in others:
        n_copy(target, t).wait_send()
        l_copy(target, t).wait_send()
    for c in started:
        c.wait_send()
    for g in (w, q, o, cl):
        g.drain()


def layer(*operands):
    vmem = pl.BlockSpec(memory_space=pltpu.VMEM)
    smem = pl.BlockSpec(memory_space=pltpu.SMEM)
    hbm = pl.BlockSpec(memory_space=pl.ANY)
    dma = pltpu.SemaphoreType.DMA
    share = TOKENS // NT
    half = SCORED // 2
    rows_dev = operands[6].shape[0]
    return pl.pallas_call(
        layer_kernel,
        out_shape=jax.ShapeDtypeStruct((share, SCORED), F32),
        in_specs=[hbm] * 7 + [smem] + [vmem] * 7,
        out_specs=vmem,
        scratch_shapes=[
            pltpu.VMEM((TOKENS, FB), BF16),
            pltpu.VMEM((2, ROWS, FB), BF16),
            pltpu.VMEM((128, WCOLS), BF16),
            pltpu.VMEM((FB, 128), BF16),
            pltpu.VMEM((rows_dev, D), BF16),
            pltpu.VMEM((3 * ROWS, FB), BF16),
            pltpu.VMEM((NT, 3 * ROWS, FB), BF16),
            pltpu.VMEM((NP, 2 * ROWS, 128), BF16),
            pltpu.VMEM((NP, 128, WCOLS), BF16),
            pltpu.VMEM((2 * ROWS, WCOLS), F32),
            pltpu.VMEM((2, ROWS, WCOLS), BF16),
            pltpu.VMEM((NP, 2, ROWS, WCOLS), BF16),
            pltpu.VMEM((NP, FB, 128), BF16),
            pltpu.VMEM((NP, 2, ROWS, FB), BF16),
            pltpu.VMEM((SEQ, FB), BF16),
            pltpu.VMEM((NT, TOKENS, FB), BF16),
            pltpu.VMEM((NT, TOKENS, FB), BF16),
            pltpu.VMEM((SEQ, SEQ), F32),
            pltpu.VMEM((SEQ, SEQ), F32),
            pltpu.VMEM((NT, SCORED, FB), BF16),
            pltpu.VMEM((NT, half, FB), BF16),
            pltpu.VMEM((NT, half, FB), BF16),
            pltpu.VMEM((NT, half, FB), BF16),
            pltpu.VMEM((4, half // 4, FB), BF16),
            pltpu.VMEM((4, half // 4, FB), BF16),
            pltpu.VMEM((4, half // 4, FB), BF16),
            pltpu.VMEM((half // 4, FB), BF16),
            pltpu.VMEM((2, 4, half // 4, FB), BF16),
            pltpu.VMEM((SEQ, FB), BF16),
            pltpu.VMEM((NT, share, 128), F32),
            pltpu.VMEM((NT, share, 128), F32),
            pltpu.VMEM((NT, share, SCORED), BF16),
            pltpu.VMEM((NT, share, SCORED), BF16),
            dma((7,)),
            dma((NT,)), dma((NT,)),
            dma((N_SENDS,)), dma((NP,)),
            dma((N_SENDS,)), dma((NP,)),
            dma((N_SENDS,)), dma((NP,)),
            dma((N_SENDS,)), dma((NP,)),
            dma((NT, PROMPTS)), dma((NT, PROMPTS)),
            dma((21,)), dma((10,)), dma((4,)), dma((4,)), dma((4,)),
            dma((NT,)), dma((NT,)), dma((NT,)), dma((NT,)),
        ],
        compiler_params=pltpu.CompilerParams(
            collective_id=0, has_side_effects=True, vmem_limit_bytes=60 * 1024 * 1024
        ),
        cost_estimate=pl.CostEstimate(
            flops=4 * 10**9, bytes_accessed=20 * 2**20, transcendentals=10**6
        ),
        name="layer",
    )(*operands)


def rope_tables():
    half = HD // 2
    exponents = -(np.arange(half, dtype=np.float32) * np.float32(2.0 / HD))
    freqs = (np.float32(THETA) ** exponents).astype(np.float32)
    angles = np.arange(SEQ, dtype=np.float32)[:, None] * freqs[None, :]
    cosine, sine = np.cos(angles), np.sin(angles)
    return (
        np.concatenate([cosine, cosine], axis=1).astype(np.float32),
        np.concatenate([-sine, sine], axis=1).astype(np.float32),
    )


def on_device(
    resid_corrupt, resid_clean, patch_level, patch_mask, norm_gain, final_gain,
    w_query, w_key, w_value, w_out, unembed, scored_ids, base_logits,
):
    cosine, sine = rope_tables()
    out = layer(
        resid_corrupt, resid_clean, w_query, w_key, w_value, w_out, unembed,
        patch_level, patch_mask, scored_ids[:, None], norm_gain[None, :], final_gain[None, :],
        jnp.asarray(cosine), jnp.asarray(sine), base_logits,
    )
    return out[None]


def solution(mesh):
    placed = (
        P(None, "tp"),
        P(None, "patch", "tp"),
        P("patch"),
        P("patch", None),
        P("tp"),
        P("tp"),
        P("patch", "tp"),
        P("patch", "tp"),
        P("patch", "tp"),
        P("tp", "patch"),
        P(("patch", "tp"), None),
        P(),
        P("tp", None),
    )
    return jax.shard_map(
        on_device, mesh=mesh, in_specs=placed, out_specs=P("patch", "tp", None), check_vma=False
    )
```

time: 318 us -> 157 us (0.49)
  the two profiles are of different devices: /device:TPU:2 before, /device:TPU:25 now
where the time goes in v2:
time: 157 us
  Pallas kernels  151 us (96%)
  local copies, waits for them, and re-layouts  5.44 us (3%)
    pallas_call x1, Pallas kernels, layer(): pl.pallas_call(layer_kernel, out_shape=jax.ShapeDtypeStruct((share, SCORE...  151 us

profile of v2, /device:TPU:25, one launch (start us, length us, event | category | flops | bytes accessed | tf_op | source)
XLA Modules:
  0.0 157.2 jit_solution(12203657361901973977)
XLA Ops:
  0.7 1.3 broadcast_in_dim.13.ngain_ref
  1.9 1.3 broadcast_in_dim.14.fgain_ref
  3.2 1.5 copy.16.ids_ref
  4.6 151.1 %layer.1 = f32[64,256]{1,0:T(8,128)} custom-call(bf16[512,512]{1,0:T(8,128)(2,1)} %corrupt_hbm.1, bf16[2,16,512]{2,1,0:T(8,128)(2,1)} %clean_hbm.1, bf16[128,512]{1,0:T(8,128)(2,1)} %wq_hbm.1, bf16[128,128]{1,0:T(8,128)(2,1)} %wk_hbm.1, bf16[128,128]{1,0:T(8,128)(2,1)} %wv_hbm.1, bf16[512,128]{1,0:T(8,128)(2,1)} %wo_hbm.1, bf16[501,4096]{1,0:T(8,128)(2,1)} %unembed_hbm.1, ...), custom_call_target="tpu_custom_call" | custom-call | flops 4000000000 | bytes 20971520 | tf_op jit(solution)/shard_map/layer/pallas_call | solution.py:433
  155.7 1.5 copy.19

commit v3 on v2

v3 whole, which is shorter than its diff:
```python
import jax
import jax.numpy as jnp
import numpy as np
from jax import lax
from jax.experimental import pallas as pl
from jax.experimental.pallas import tpu as pltpu
from jax.sharding import PartitionSpec as P

D = 4096
HD = 128
SEQ = 128
PROMPTS = 4
TOKENS = PROMPTS * SEQ
SCORED = 256
NP = 32
NT = 8
FB = D // NT
ROWS = TOKENS // NP
QCOLS = 512
KVCOL = 128
WCOLS = QCOLS + 2 * KVCOL
EPSILON = 1e-05
THETA = 500000.0
MESH = pl.DeviceIdType.MESH
F32 = jnp.float32
BF16 = jnp.bfloat16
N_SENDS = 31


class PatchGather:
    def __init__(self, own, buf, send, recv):
        self.own, self.buf, self.send, self.recv = own, buf, send, recv
        me = lax.axis_index("patch")
        self.me = me
        self.x, self.z, self.c = me // 8, (me // 2) % 4, me % 2
        self.way = 1 - 2 * self.c
        self.started = []

    def block(self, dx, dz, other=False):
        c = 1 - self.c if other else self.c
        return ((self.x + dx) % 4) * 8 + ((self.z + dz + 4) % 4) * 2 + c

    def copy(self, src, index, target, slot):
        return pltpu.make_async_remote_copy(
            src_ref=src,
            dst_ref=self.buf.at[index],
            send_sem=self.send.at[slot],
            recv_sem=self.recv.at[index],
            device_id={"patch": target},
            device_id_type=MESH,
        )

    def start(self, src, index, target):
        c = self.copy(src, index, target, len(self.started))
        c.start()
        self.started.append(c)

    def wait(self, index):
        self.copy(self.buf.at[index], index, self.block(1, 0), 0).wait_recv()

    def z_send(self):
        for dz in (self.way, -self.way):
            self.start(self.own, self.me, self.block(0, dz))

    def own_send(self):
        for target in (self.block(1, 0), self.block(3, 0), self.block(0, 0, True)):
            self.start(self.own, self.me, target)

    def z_relay(self):
        b = self.block(0, -self.way)
        self.wait(b)
        self.start(self.buf.at[b], b, self.block(0, self.way))

    def spread(self, b):
        for target in (self.block(1, 0), self.block(3, 0), self.block(0, 0, True)):
            self.start(self.buf.at[b], b, target)

    def z_forward(self, relayed=False):
        for k, dz in enumerate((-self.way, self.way, 2)):
            b = self.block(0, dz)
            if k > 0:
                self.wait(b)
            elif not relayed:
                self.z_relay()
            self.spread(b)
            if k == 0 and not relayed:
                self.x_near(0)

    def x_near(self, k, then=None):
        for dx in (3, 1):
            b = self.block(dx, (0, -self.way, self.way, 2)[k])
            self.wait(b)
            if (k < 2) == (dx == 3):
                self.start(self.buf.at[b], b, self.block(4 - dx, 0))
            self.start(self.buf.at[b], b, self.block(0, 0, True))
            if then is not None:
                then(b)

    def x_forward(self, then=None, first=1):
        for k in range(first, 4):
            self.x_near(k, then)

    def far(self, then=None):
        for dz in (0, -self.way, self.way, 2):
            b = self.block(2, dz)
            self.wait(b)
            self.start(self.buf.at[b], b, self.block(0, 0, True))
            if then is not None:
                then(b)

    def core_wait(self, then=None):
        z = (0, self.way, -self.way, 2)
        for dx, dz in [(0, dz) for dz in z] + [(dx, dz) for dz in z for dx in (3, 1)] + [(2, dz) for dz in z]:
            b = self.block(dx, dz, True)
            self.wait(b)
            if then is not None:
                then(b)

    def drain(self):
        for c in self.started:
            c.wait_send()


def layer_kernel(
    corrupt_hbm, clean_hbm, wq_hbm, wk_hbm, wv_hbm, wo_hbm, unembed_hbm,
    level_ref, mask_ref, ids_ref, gains_ref, cos_ref, sin_ref,
    out_ref,
    corrupt_ref, clean_ref, w_ref, wo_ref, wo_own, unembed_ref,
    xin, xrecv, nbuf, wbuf, acc, qown, qbuf, obuf, cbuf, att, head, early_ref, late_ref,
    chosen, chosen_got, paired, spread, mine, mine_got, spread_z, sum_z, sum_x, own_x, score, fin, score_t, squares, ssq, ssq_got, lg, lg_got,
    local, x_send, x_recv, w_send, w_recv, q_send, q_recv, o_send, o_recv, c_send, c_recv, a_send, a_recv,
    s_send, s_recv, sz_recv, sx_recv, sg_recv, l_send, l_recv, n_send, n_recv,
):
    t = lax.axis_index("tp")
    w = PatchGather(w_ref, wbuf, w_send, w_recv)
    q = PatchGather(qown, qbuf, q_send, q_recv)
    o = PatchGather(wo_own, obuf, o_send, o_recv)
    cl = PatchGather(clean_ref, cbuf, c_send, c_recv)
    me, px, pz, pc = w.me, w.x, w.z, w.c
    ty, tz = t // 2, t % 2
    beside = t + 1 - 2 * tz
    others = [(t + k) % NT for k in range(1, NT)]
    z_others = [(k, (pz + k) % 4) for k in (1, 3, 2)]
    x_others = [(k, (px + k) % 4) for k in (1, 3, 2)]
    partner = w.block(0, 0, True)
    swap_p, swap_t = 4 * t + me % 4, me // 4
    swaps = swap_t != t

    loads = [
        pltpu.make_async_copy(src, dst, local.at[k])
        for k, (src, dst) in enumerate(
            [
                (corrupt_hbm, corrupt_ref),
                (clean_hbm, clean_ref),
                (wq_hbm, w_ref.at[:, pl.ds(0, QCOLS)]),
                (wk_hbm, w_ref.at[:, pl.ds(QCOLS, KVCOL)]),
                (wv_hbm, w_ref.at[:, pl.ds(QCOLS + KVCOL, KVCOL)]),
                (wo_hbm, wo_ref),
                (unembed_hbm, unembed_ref),
            ]
        )
    ]
    for c in loads:
        c.start()
    barrier = pltpu.get_barrier_semaphore()
    peers = (
        [{"tp": k} for k in others]
        + [{"patch": w.block(0, dz)} for dz in (1, 3, 2)]
        + [{"patch": w.block(dx, 0)} for dx in (1, 3, 2)]
        + [{"patch": partner}]
    )
    for peer in peers:
        pl.semaphore_signal(barrier, inc=1, device_id=peer, device_id_type=MESH)

    @pl.when(swaps)
    def _():
        pl.semaphore_signal(
            barrier, inc=1, device_id={"patch": swap_p, "tp": swap_t}, device_id_type=MESH
        )

    for c in loads[:2]:
        c.wait()
    xin[:ROWS] = corrupt_ref[pl.ds(pl.multiple_of(me * ROWS, ROWS), ROWS), :]
    xin[ROWS : 2 * ROWS] = clean_ref[0]
    xin[2 * ROWS :] = jnp.broadcast_to(gains_ref[:1], (ROWS, FB)).astype(BF16)
    xrecv[t] = xin[...]
    spliced = jnp.transpose(jnp.broadcast_to(mask_ref[...].astype(F32), (SEQ, SEQ)))
    level = level_ref[0].astype(F32)
    early_ref[...] = spliced * (1.0 - level)
    late_ref[...] = spliced * level
    cbuf[me] = clean_ref[...]
    for c in loads[2:6]:
        c.wait()
    pl.semaphore_wait(barrier, len(peers) + swaps.astype(jnp.int32))

    started = []

    def begin(c):
        c.start()
        started.append(c)

    def x_copy(k, target, to):
        return pltpu.make_async_remote_copy(
            src_ref=xin, dst_ref=xrecv.at[to], send_sem=x_send.at[k], recv_sem=x_recv.at[to],
            device_id={"tp": target}, device_id_type=MESH,
        )

    def s_copy(src, dst, send, recv, where):
        return pltpu.make_async_remote_copy(
            src_ref=src, dst_ref=dst, send_sem=s_send.at[send], recv_sem=recv,
            device_id=where, device_id_type=MESH,
        )

    w.z_send()
    w.own_send()
    for k, target in enumerate(others):
        begin(x_copy(k, target, t))
    swap = s_copy(wo_ref, wo_own, 21, s_recv.at[10], {"patch": swap_p, "tp": swap_t})

    @pl.when(swaps)
    def _():
        swap.start()

    loads[6].wait()
    rows_dev = unembed_ref.shape[0]
    wanted = jnp.transpose(jnp.broadcast_to(ids_ref[...].astype(F32), (SCORED, SCORED)))[:, :1]
    wanted = wanted.astype(jnp.int32) - (me * NT + t) * rows_dev
    owned = jnp.where(
        wanted == lax.broadcasted_iota(jnp.int32, (SCORED, rows_dev), 1), 1.0, 0.0
    ).astype(BF16)
    for k in range(NT):
        chosen[k] = jnp.dot(
            owned, unembed_ref[:, FB * k : FB * (k + 1)], preferred_element_type=F32
        ).astype(BF16)
    half = SCORED // 2
    pair = s_copy(
        chosen.at[:, pl.ds(pl.multiple_of(half * (1 - pc), half), half)],
        chosen_got, 0, s_recv.at[0], {"patch": partner},
    )
    begin(pair)
    pair.wait_recv()
    paired[...] = (
        chosen[:, pl.ds(pl.multiple_of(half * pc, half), half)] + chosen_got[...]
    ).reshape(4, 2, half, FB)
    y_others = [(k, (ty + k) % 4) for k in (1, 3, 2)]
    for k, y in y_others:
        begin(s_copy(paired.at[y], spread.at[ty], k, s_recv.at[1 + ty], {"tp": 2 * y + tz}))

    w.z_forward()

    @pl.when(swaps)
    def _():
        swap.wait_recv()

    @pl.when(jnp.logical_not(swaps))
    def _():
        wo_own[...] = wo_ref[...]

    o.z_send()
    for target in others:
        x_copy(0, target, target).wait_recv()
    total = jnp.zeros((2 * ROWS, 1), F32)
    for k in range(NT):
        v = xrecv[k, : 2 * ROWS, :].astype(F32)
        total = total + jnp.sum(v * v, axis=1, keepdims=True)
    scale = lax.rsqrt(total / D + EPSILON)
    for k in range(NT):
        v = xrecv[k, : 2 * ROWS, :].astype(F32)
        g = xrecv[k, 2 * ROWS :, :].astype(F32)[:1]
        v = (v * scale * g).astype(BF16)
        for j in range(4):
            nbuf[4 * k + j] = v[:, 128 * j : 128 * (j + 1)]

    acc[...] = jnp.dot(nbuf[me], w_ref[...], preferred_element_type=F32)

    def add(b):
        acc[...] += jnp.dot(nbuf[b], wbuf[b], preferred_element_type=F32)

    for b in [w.block(0, dz) for dz in (3, 1, 2)] + [w.block(dx, 0) for dx in (3, 1)]:
        add(b)
    w.x_forward(add)
    obuf[me] = wo_own[...]
    o.z_relay()
    cl.z_send()

    v = paired[ty]
    for k, y in y_others:
        s_copy(paired.at[y], spread.at[y], 0, s_recv.at[1 + y], {"tp": 2 * y + tz}).wait_recv()
        v = v + spread[y]
    mine[...] = v
    begin(s_copy(mine.at[1 - tz], mine_got, 4, s_recv.at[5], {"tp": beside}))
    w.far(add)
    w.core_wait(add)

    at = pl.ds(pl.multiple_of((me * ROWS) % SEQ, ROWS), ROWS)
    cosine = jnp.concatenate([cos_ref[at, :]] * 2, axis=0)
    sine = jnp.concatenate([sin_ref[at, :]] * 2, axis=0)
    for h in range(WCOLS // HD):
        v = acc[:, HD * h : HD * (h + 1)]
        if h < 5:
            v = v * cosine + pltpu.roll(v, HD // 2, 1) * sine
        v = v.astype(BF16)
        for s in range(2):
            qown[s, :, HD * h : HD * (h + 1)] = v[ROWS * s : ROWS * (s + 1)]
    qbuf[me] = qown[...]
    q.z_send()
    q.own_send()
    cl.z_relay()
    q.z_forward()

    s_copy(mine.at[1 - tz], mine_got, 4, s_recv.at[5], {"tp": beside}).wait_recv()
    spread_z[...] = (mine[tz] + mine_got[...]).reshape(4, half // 4, FB)
    for k, target in z_others:
        begin(s_copy(spread_z.at[target], sum_z.at[pz], 8 + k, sz_recv.at[pz], {"patch": w.block(0, k)}))

    q.x_forward()
    o.own_send()
    o.z_forward(True)
    cl.own_send()
    cl.z_forward(True)
    q.far()

    v = spread_z[pz]
    for k, target in z_others:
        s_copy(spread_z.at[target], sum_z.at[target], 0, sz_recv.at[target], {"patch": w.block(0, k)}).wait_recv()
        v = v + sum_z[target]
    own_x[...] = v
    for k, target in x_others:
        begin(s_copy(own_x, sum_x.at[px], 12 + k, sx_recv.at[px], {"patch": w.block(k, 0)}))

    q.core_wait()

    early = early_ref[...] > 0.5
    row = lax.broadcasted_iota(jnp.int32, (4 * SEQ, SEQ), 0) % SEQ
    col = lax.broadcasted_iota(jnp.int32, (4 * SEQ, SEQ), 1)
    causal = row >= col

    def a_copy(index, n, source, target):
        rows = pl.ds(SEQ * n, SEQ)
        return pltpu.make_async_remote_copy(
            src_ref=att.at[source, rows], dst_ref=att.at[source, rows],
            send_sem=a_send.at[index], recv_sem=a_recv.at[source, n],
            device_id={"tp": target}, device_id_type=MESH,
        )

    a_count = []

    def a_start(n, source, target):
        begin(a_copy(len(a_count), n, source, target))
        a_count.append(n)

    def a_wait(n, source):
        a_copy(0, n, source, others[0]).wait_recv()

    up, down, far_y = ((ty + 1) % 4) * 2, ((ty + 3) % 4) * 2, ((ty + 2) % 4) * 2
    near = (down, up)

    def across(n):
        return n >= 2

    def clockwise(n):
        return n % 2 == 0

    def first(n):
        for y in near:
            a_wait(n, y + tz)
            if clockwise(n) == (y is down):
                a_start(n, y + tz, (up if y is down else down) + tz)
            if across(n):
                a_start(n, y + tz, beside)
        a_wait(n, beside)
        if not across(n):
            a_start(n, beside, up + tz)
            a_start(n, beside, down + tz)

    def second(n):
        a_wait(n, far_y + tz)
        if across(n):
            a_start(n, far_y + tz, beside)
        for y in near:
            a_wait(n, y + 1 - tz)
            if not across(n) and clockwise(n) == (y is down):
                a_start(n, y + 1 - tz, (up if y is down else down) + tz)

    def third(n):
        a_wait(n, far_y + 1 - tz)

    for n in range(PROMPTS):
        def picked(lo, hi, n=n):
            a = qbuf[8 * n : 8 * (n + 1), 0, :, lo:hi].reshape(SEQ, hi - lo).astype(F32)
            b = qbuf[8 * n : 8 * (n + 1), 1, :, lo:hi].reshape(SEQ, hi - lo).astype(F32)
            return jnp.where(early, b, a).astype(BF16)

        queries = jnp.concatenate([picked(HD * h, HD * (h + 1)) for h in range(4)], axis=0)
        keys = picked(QCOLS, QCOLS + HD)
        values = picked(QCOLS + HD, QCOLS + 2 * HD)
        scores = lax.dot_general(
            queries, keys, (((1,), (1,)), ((), ())), preferred_element_type=F32
        ) * HD ** (-0.5)
        scores = jnp.where(causal, scores, -1e30)
        scores = jnp.exp(scores - jnp.max(scores, axis=1, keepdims=True))
        probs = (scores / jnp.sum(scores, axis=1, keepdims=True)).astype(BF16)
        heads = jnp.dot(probs, values, preferred_element_type=F32).astype(BF16)
        for h in range(4):
            att[t, SEQ * n : SEQ * (n + 1), HD * h : HD * (h + 1)] = heads[SEQ * h : SEQ * (h + 1)]
        for target in (up + tz, down + tz, beside):
            a_start(n, t, target)

    gain = gains_ref[1:]
    share = TOKENS // NT

    def l_copy(target, to):
        return pltpu.make_async_remote_copy(
            src_ref=lg.at[target], dst_ref=lg_got.at[to], send_sem=l_send.at[target], recv_sem=l_recv.at[to],
            device_id={"tp": target}, device_id_type=MESH,
        )

    def n_copy(target, to):
        return pltpu.make_async_remote_copy(
            src_ref=ssq.at[target], dst_ref=ssq_got.at[to], send_sem=n_send.at[target], recv_sem=n_recv.at[to],
            device_id={"tp": target}, device_id_type=MESH,
        )

    last = far_y + 1 - tz

    def project(n, source):
        block = jnp.concatenate([obuf[4 * source + k] for k in range(4)], axis=1)
        head[n] += jnp.dot(att[source, SEQ * n : SEQ * (n + 1)], block, preferred_element_type=F32)

    def project_most(n):
        head[n] = jnp.zeros((SEQ, FB), F32)

        def one(k, carry):
            project(n, (last + 1 + k) % NT)
            return carry

        lax.fori_loop(0, NT - 1, one, 0)

    first(0)
    o.x_forward(first=0)

    v = own_x[...]
    for k, target in x_others:
        s_copy(own_x, sum_x.at[target], 0, sx_recv.at[target], {"patch": w.block(k, 0)}).wait_recv()
        v = v + sum_x[target]
    score[pc, pz] = v
    for k, target in z_others:
        begin(s_copy(score.at[pc, pz], score.at[pc, pz], 16 + k, sg_recv.at[pz], {"patch": w.block(0, k)}))

    first(1)
    first(2)
    o.far()
    cl.x_forward(first=0)
    first(3)
    for k, target in z_others:
        s_copy(score.at[pc, target], score.at[pc, target], 0, sg_recv.at[target], {"patch": w.block(0, k)}).wait_recv()
    begin(s_copy(score.at[pc], score.at[pc], 20, s_recv.at[9], {"patch": partner}))
    second(0)
    cl.far()
    second(1)
    o.core_wait()
    project_most(0)
    second(2)
    s_copy(score.at[pc], score.at[1 - pc], 0, s_recv.at[9], {"patch": partner}).wait_recv()
    score_t[...] = jnp.transpose(score[...].reshape(SCORED, FB).astype(F32)).astype(BF16)
    project_most(1)
    second(3)
    cl.core_wait()

    gain = gains_ref[1:]
    share = TOKENS // NT

    def l_copy(target, to):
        return pltpu.make_async_remote_copy(
            src_ref=lg.at[target], dst_ref=lg_got.at[to], send_sem=l_send.at[target], recv_sem=l_recv.at[to],
            device_id={"tp": target}, device_id_type=MESH,
        )

    def n_copy(target, to):
        return pltpu.make_async_remote_copy(
            src_ref=ssq.at[target // 2], dst_ref=ssq_got.at[to], send_sem=n_send.at[target], recv_sem=n_recv.at[to],
            device_id={"tp": target}, device_id_type=MESH,
        )

    for n in range(PROMPTS):
        if n >= 2:
            project_most(n)
        third(n)
        project(n, last)

        def finish(i, carry, n=n):
            at = pl.ds(pl.multiple_of(SEQ * n + ROWS * i, ROWS), ROWS)
            local_at = pl.ds(pl.multiple_of(ROWS * i, ROWS), ROWS)
            e = early_ref[local_at, :1] > 0.5
            late = late_ref[local_at, :1] > 0.5
            v = corrupt_ref[at, :].astype(F32)
            v = jnp.where(e, cbuf[8 * n + i, 0].astype(F32), v)
            v = v + head[n, local_at, :]
            v = jnp.where(late, cbuf[8 * n + i, 1].astype(F32), v)
            squares[local_at, :] = jnp.broadcast_to(
                jnp.sum(v * v, axis=1, keepdims=True), (ROWS, 128)
            )
            fin[local_at, :] = (v * gain).astype(BF16)
            return carry

        lax.fori_loop(0, SEQ // ROWS, finish, 0)
        ssq[n] = jnp.transpose(squares[...])[:8]
        value = jnp.dot(fin[...], score_t[...], preferred_element_type=F32).astype(BF16)
        for s in range(2):
            target = 2 * n + s
            lg[target] = value[share * s : share * (s + 1)]

            @pl.when(target != t)
            def _(target=target):
                n_copy(target, t).start()
                l_copy(target, t).start()

    logits = lg[t].astype(F32)
    total = ssq[ty]
    for target in others:
        n_copy(target, target).wait_recv()
        l_copy(target, target).wait_recv()
        logits = logits + lg_got[target].astype(F32)
        total = total + ssq_got[target]
    scale = jnp.transpose(jnp.broadcast_to(lax.rsqrt(total[:1] / D + EPSILON), (SEQ, SEQ)))
    scale = jnp.where(tz == 0, scale[:share], scale[share:])
    out_ref[...] = logits * scale[:, :1]

    for target in others:
        n_copy(target, t).wait_send()
        l_copy(target, t).wait_send()

    @pl.when(swaps)
    def _():
        swap.wait_send()

    for c in started:
        c.wait_send()
    for g in (w, q, o, cl):
        g.drain()


def layer(*operands):
    vmem = pl.BlockSpec(memory_space=pltpu.VMEM)
    smem = pl.BlockSpec(memory_space=pltpu.SMEM)
    hbm = pl.BlockSpec(memory_space=pl.ANY)
    dma = pltpu.SemaphoreType.DMA
    share = TOKENS // NT
    half = SCORED // 2
    rows_dev = operands[6].shape[0]
    return pl.pallas_call(
        layer_kernel,
        out_shape=jax.ShapeDtypeStruct((share, SCORED), F32),
        in_specs=[hbm] * 7 + [smem] + [vmem] * 5,
        out_specs=vmem,
        scratch_shapes=[
            pltpu.VMEM((TOKENS, FB), BF16),
            pltpu.VMEM((2, ROWS, FB), BF16),
            pltpu.VMEM((128, WCOLS), BF16),
            pltpu.VMEM((FB, 128), BF16),
            pltpu.VMEM((FB, 128), BF16),
            pltpu.VMEM((rows_dev, D), BF16),
            pltpu.VMEM((3 * ROWS, FB), BF16),
            pltpu.VMEM((NT, 3 * ROWS, FB), BF16),
            pltpu.VMEM((NP, 2 * ROWS, 128), BF16),
            pltpu.VMEM((NP, 128, WCOLS), BF16),
            pltpu.VMEM((2 * ROWS, WCOLS), F32),
            pltpu.VMEM((2, ROWS, WCOLS), BF16),
            pltpu.VMEM((NP, 2, ROWS, WCOLS), BF16),
            pltpu.VMEM((NP, FB, 128), BF16),
            pltpu.VMEM((NP, 2, ROWS, FB), BF16),
            pltpu.VMEM((NT, TOKENS, FB), BF16),
            pltpu.VMEM((PROMPTS, SEQ, FB), F32),
            pltpu.VMEM((SEQ, SEQ), F32),
            pltpu.VMEM((SEQ, SEQ), F32),
            pltpu.VMEM((NT, SCORED, FB), BF16),
            pltpu.VMEM((NT, half, FB), BF16),
            pltpu.VMEM((4, 2, half, FB), BF16),
            pltpu.VMEM((4, 2, half, FB), BF16),
            pltpu.VMEM((2, half, FB), BF16),
            pltpu.VMEM((half, FB), BF16),
            pltpu.VMEM((4, half // 4, FB), BF16),
            pltpu.VMEM((4, half // 4, FB), BF16),
            pltpu.VMEM((4, half // 4, FB), BF16),
            pltpu.VMEM((half // 4, FB), BF16),
            pltpu.VMEM((2, 4, half // 4, FB), BF16),
            pltpu.VMEM((SEQ, FB), BF16),
            pltpu.VMEM((FB, SCORED), BF16),
            pltpu.VMEM((SEQ, 128), F32),
            pltpu.VMEM((PROMPTS, 8, 128), F32),
            pltpu.VMEM((NT, 8, 128), F32),
            pltpu.VMEM((NT, share, SCORED), BF16),
            pltpu.VMEM((NT, share, SCORED), BF16),
            dma((7,)),
            dma((NT,)), dma((NT,)),
            dma((N_SENDS,)), dma((NP,)),
            dma((N_SENDS,)), dma((NP,)),
            dma((N_SENDS,)), dma((NP,)),
            dma((N_SENDS,)), dma((NP,)),
            dma((32,)), dma((NT, PROMPTS)),
            dma((22,)), dma((11,)), dma((4,)), dma((4,)), dma((4,)),
            dma((NT,)), dma((NT,)), dma((NT,)), dma((NT,)),
        ],
        compiler_params=pltpu.CompilerParams(
            collective_id=0, has_side_effects=True, vmem_limit_bytes=60 * 1024 * 1024
        ),
        cost_estimate=pl.CostEstimate(
            flops=4 * 10**9, bytes_accessed=20 * 2**20, transcendentals=10**6
        ),
        name="layer",
    )(*operands)


def rope_tables():
    half = HD // 2
    exponents = -(np.arange(half, dtype=np.float32) * np.float32(2.0 / HD))
    freqs = (np.float32(THETA) ** exponents).astype(np.float32)
    angles = np.arange(SEQ, dtype=np.float32)[:, None] * freqs[None, :]
    cosine, sine = np.cos(angles), np.sin(angles)
    return (
        np.concatenate([cosine, cosine], axis=1).astype(np.float32),
        np.concatenate([-sine, sine], axis=1).astype(np.float32),
    )


def on_device(
    resid_corrupt, resid_clean, patch_level, patch_mask, norm_gain, final_gain,
    w_query, w_key, w_value, w_out, unembed, scored_ids, base_logits,
):
    cosine, sine = rope_tables()
    gains = jnp.stack([norm_gain, final_gain]).astype(F32)
    out = layer(
        resid_corrupt, resid_clean, w_query, w_key, w_value, w_out, unembed,
        patch_level, patch_mask, scored_ids[None, :], gains, jnp.asarray(cosine), jnp.asarray(sine),
    )
    return (out - base_logits)[None]


def solution(mesh):
    placed = (
        P(None, "tp"),
        P(None, "patch", "tp"),
        P("patch"),
        P("patch", None),
        P("tp"),
        P("tp"),
        P("patch", "tp"),
        P("patch", "tp"),
        P("patch", "tp"),
        P("tp", "patch"),
        P(("patch", "tp"), None),
        P(),
        P("tp", None),
    )
    return jax.shard_map(
        on_device, mesh=mesh, in_specs=placed, out_specs=P("patch", "tp", None), check_vma=False
    )
```

time: 157 us -> 119 us (0.76)
  the two profiles are of different devices: /device:TPU:25 before, /device:TPU:2 now
where the time goes in v3:
time: 119 us; the launch traced here: 117 us
  Pallas kernels  113 us (95%)
  other arithmetic  2.08 us (2%)
  local copies, waits for them, and re-layouts  1.37 us (1%)
    pallas_call x1, Pallas kernels, layer(): pl.pallas_call(layer_kernel, out_shape=jax.ShapeDtypeStruct((share, SCORE...  113 us

profile of v3, /device:TPU:2, one launch (start us, length us, event | category | flops | bytes accessed | tf_op | source)
XLA Modules:
  0.0 116.8 jit_solution(6323106928437946905)
XLA Ops:
  0.7 0.7 stack.9
  1.3 0.7 stack.10
  2.0 0.6 maximum_convert_fusion.gains_ref
  2.6 0.0 copy-start
  2.6 112.7 %layer.1 = f32[64,256]{1,0:T(8,128)} custom-call(bf16[512,512]{1,0:T(8,128)(2,1)} %corrupt_hbm.1, bf16[2,16,512]{2,1,0:T(8,128)(2,1)} %clean_hbm.1, bf16[128,512]{1,0:T(8,128)(2,1)} %wq_hbm.1, bf16[128,128]{1,0:T(8,128)(2,1)} %wk_hbm.1, bf16[128,128]{1,0:T(8,128)(2,1)} %wv_hbm.1, bf16[512,128]{1,0:T(8,128)(2,1)} %wo_hbm.1, bf16[501,4096]{1,0:T(8,128)(2,1)} %unembed_hbm.1, ...), custom_call_target="tpu_custom_call" | custom-call | flops 4000000000 | bytes 20971520 | tf_op jit(solution)/shard_map/layer/pallas_call | solution.py:551
  115.3 0.0 copy-done
  115.3 1.5 %subtract_bitcast_fusion = f32[1,64,256]{2,1,0:T(8,128)} fusion(f32[64,256]{1,0:T(8,128)} %layer.1, f32[64,256]{1,0:T(8,128)S(1)} %copy-done), kind=kLoop, calls=%fused_computation | loop fusion | flops 16384 | bytes 196608 | tf_op jit(solution)/shard_map/broadcast_in_dim | solution.py:636
Async XLA Ops:
  2.6 112.7 %copy-start = (f32[64,256]{1,0:T(8,128)S(1)}, f32[64,256]{1,0:T(8,128)}, u32[]{:S(2)}) copy-start(f32[64,256]{1,0:T(8,128)} %param.27) | copy-start | bytes 196612

commit v4 on v3

--- a/solution.py
+++ b/solution.py
@@ -76,21 +76,19 @@
             self.start(self.buf.at[b], b, target)
 
     def z_forward(self, relayed=False):
+        if not relayed:
+            self.z_relay()
         for k, dz in enumerate((-self.way, self.way, 2)):
             b = self.block(0, dz)
             if k > 0:
                 self.wait(b)
-            elif not relayed:
-                self.z_relay()
             self.spread(b)
-            if k == 0 and not relayed:
-                self.x_near(0)
 
     def x_near(self, k, then=None):
         for dx in (3, 1):
             b = self.block(dx, (0, -self.way, self.way, 2)[k])
             self.wait(b)
-            if (k < 2) == (dx == 3):
+            if (k in (0, 3)) == (dx == 3):
                 self.start(self.buf.at[b], b, self.block(4 - dx, 0))
             self.start(self.buf.at[b], b, self.block(0, 0, True))
             if then is not None:
@@ -108,13 +106,13 @@
             if then is not None:
                 then(b)
 
-    def core_wait(self, then=None):
-        z = (0, self.way, -self.way, 2)
-        for dx, dz in [(0, dz) for dz in z] + [(dx, dz) for dz in z for dx in (3, 1)] + [(2, dz) for dz in z]:
-            b = self.block(dx, dz, True)
-            self.wait(b)
-            if then is not None:
-                then(b)
+    def core_wait(self, then=None, steps=(0, 3, 1, 2)):
+        for dx in steps:
+            for dz in (0, self.way, -self.way, 2):
+                b = self.block(dx, dz, True)
+                self.wait(b)
+                if then is not None:
+                    then(b)
 
     def drain(self):
         for c in self.started:
@@ -123,7 +121,7 @@
 
 def layer_kernel(
     corrupt_hbm, clean_hbm, wq_hbm, wk_hbm, wv_hbm, wo_hbm, unembed_hbm,
-    level_ref, mask_ref, ids_ref, gains_ref, cos_ref, sin_ref,
+    level_ref, mask_ref, ids_ref, ngain_ref, fgain_ref, cos_ref, sin_ref,
     out_ref,
     corrupt_ref, clean_ref, w_ref, wo_ref, wo_own, unembed_ref,
     xin, xrecv, nbuf, wbuf, acc, qown, qbuf, obuf, cbuf, att, head, early_ref, late_ref,
@@ -182,7 +180,7 @@
         c.wait()
     xin[:ROWS] = corrupt_ref[pl.ds(pl.multiple_of(me * ROWS, ROWS), ROWS), :]
     xin[ROWS : 2 * ROWS] = clean_ref[0]
-    xin[2 * ROWS :] = jnp.broadcast_to(gains_ref[:1], (ROWS, FB)).astype(BF16)
+    xin[2 * ROWS :] = jnp.broadcast_to(ngain_ref[...].astype(F32).reshape(1, FB), (ROWS, FB)).astype(BF16)
     xrecv[t] = xin[...]
     spliced = jnp.transpose(jnp.broadcast_to(mask_ref[...].astype(F32), (SEQ, SEQ)))
     level = level_ref[0].astype(F32)
@@ -246,6 +244,7 @@
     for k, y in y_others:
         begin(s_copy(paired.at[y], spread.at[ty], k, s_recv.at[1 + ty], {"tp": 2 * y + tz}))
 
+    w.x_near(0)
     w.z_forward()
 
     @pl.when(swaps)
@@ -271,6 +270,13 @@
         for j in range(4):
             nbuf[4 * k + j] = v[:, 128 * j : 128 * (j + 1)]
 
+    v = paired[ty]
+    for k, y in y_others:
+        s_copy(paired.at[y], spread.at[y], 0, s_recv.at[1 + y], {"tp": 2 * y + tz}).wait_recv()
+        v = v + spread[y]
+    mine[...] = v
+    begin(s_copy(mine.at[1 - tz], mine_got, 4, s_recv.at[5], {"tp": beside}))
+
     acc[...] = jnp.dot(nbuf[me], w_ref[...], preferred_element_type=F32)
 
     def add(b):
@@ -283,12 +289,11 @@
     o.z_relay()
     cl.z_send()
 
-    v = paired[ty]
-    for k, y in y_others:
-        s_copy(paired.at[y], spread.at[y], 0, s_recv.at[1 + y], {"tp": 2 * y + tz}).wait_recv()
-        v = v + spread[y]
-    mine[...] = v
-    begin(s_copy(mine.at[1 - tz], mine_got, 4, s_recv.at[5], {"tp": beside}))
+    s_copy(mine.at[1 - tz], mine_got, 4, s_recv.at[5], {"tp": beside}).wait_recv()
+    spread_z[...] = (mine[tz] + mine_got[...]).reshape(4, half // 4, FB)
+    for k, target in z_others:
+        begin(s_copy(spread_z.at[target], sum_z.at[pz], 8 + k, sz_recv.at[pz], {"patch": w.block(0, k)}))
+
     w.far(add)
     w.core_wait(add)
 
@@ -305,30 +310,6 @@
     qbuf[me] = qown[...]
     q.z_send()
     q.own_send()
-    cl.z_relay()
-    q.z_forward()
-
-    s_copy(mine.at[1 - tz], mine_got, 4, s_recv.at[5], {"tp": beside}).wait_recv()
-    spread_z[...] = (mine[tz] + mine_got[...]).reshape(4, half // 4, FB)
-    for k, target in z_others:
-        begin(s_copy(spread_z.at[target], sum_z.at[pz], 8 + k, sz_recv.at[pz], {"patch": w.block(0, k)}))
-
-    q.x_forward()
-    o.own_send()
-    o.z_forward(True)
-    cl.own_send()
-    cl.z_forward(True)
-    q.far()
-
-    v = spread_z[pz]
-    for k, target in z_others:
-        s_copy(spread_z.at[target], sum_z.at[target], 0, sz_recv.at[target], {"patch": w.block(0, k)}).wait_recv()
-        v = v + sum_z[target]
-    own_x[...] = v
-    for k, target in x_others:
-        begin(s_copy(own_x, sum_x.at[px], 12 + k, sx_recv.at[px], {"patch": w.block(k, 0)}))
-
-    q.core_wait()
 
     early = early_ref[...] > 0.5
     row = lax.broadcasted_iota(jnp.int32, (4 * SEQ, SEQ), 0) % SEQ
@@ -356,7 +337,7 @@
     near = (down, up)
 
     def across(n):
-        return n >= 2
+        return n < 2
 
     def clockwise(n):
         return n % 2 == 0
@@ -377,6 +358,8 @@
         a_wait(n, far_y + tz)
         if across(n):
             a_start(n, far_y + tz, beside)
+
+    def crossed(n):
         for y in near:
             a_wait(n, y + 1 - tz)
             if not across(n) and clockwise(n) == (y is down):
@@ -385,10 +368,14 @@
     def third(n):
         a_wait(n, far_y + 1 - tz)
 
-    for n in range(PROMPTS):
-        def picked(lo, hi, n=n):
-            a = qbuf[8 * n : 8 * (n + 1), 0, :, lo:hi].reshape(SEQ, hi - lo).astype(F32)
-            b = qbuf[8 * n : 8 * (n + 1), 1, :, lo:hi].reshape(SEQ, hi - lo).astype(F32)
+    prompts = [(px + dx) % 4 for dx in (0, 3, 1, 2)]
+
+    def attend(n):
+        prompt = prompts[n]
+
+        def picked(lo, hi):
+            a = qbuf[pl.ds(8 * prompt, 8), 0, :, lo:hi].reshape(SEQ, hi - lo).astype(F32)
+            b = qbuf[pl.ds(8 * prompt, 8), 1, :, lo:hi].reshape(SEQ, hi - lo).astype(F32)
             return jnp.where(early, b, a).astype(BF16)
 
         queries = jnp.concatenate([picked(HD * h, HD * (h + 1)) for h in range(4)], axis=0)
@@ -406,38 +393,27 @@
         for target in (up + tz, down + tz, beside):
             a_start(n, t, target)
 
-    gain = gains_ref[1:]
-    share = TOKENS // NT
-
-    def l_copy(target, to):
-        return pltpu.make_async_remote_copy(
-            src_ref=lg.at[target], dst_ref=lg_got.at[to], send_sem=l_send.at[target], recv_sem=l_recv.at[to],
-            device_id={"tp": target}, device_id_type=MESH,
-        )
-
-    def n_copy(target, to):
-        return pltpu.make_async_remote_copy(
-            src_ref=ssq.at[target], dst_ref=ssq_got.at[to], send_sem=n_send.at[target], recv_sem=n_recv.at[to],
-            device_id={"tp": target}, device_id_type=MESH,
-        )
-
-    last = far_y + 1 - tz
-
-    def project(n, source):
-        block = jnp.concatenate([obuf[4 * source + k] for k in range(4)], axis=1)
-        head[n] += jnp.dot(att[source, SEQ * n : SEQ * (n + 1)], block, preferred_element_type=F32)
-
-    def project_most(n):
-        head[n] = jnp.zeros((SEQ, FB), F32)
-
-        def one(k, carry):
-            project(n, (last + 1 + k) % NT)
-            return carry
-
-        lax.fori_loop(0, NT - 1, one, 0)
-
-    first(0)
-    o.x_forward(first=0)
+    q.z_forward()
+    q.x_near(0)
+    q.core_wait(steps=(0,))
+    attend(0)
+
+    v = spread_z[pz]
+    for k, target in z_others:
+        s_copy(spread_z.at[target], sum_z.at[target], 0, sz_recv.at[target], {"patch": w.block(0, k)}).wait_recv()
+        v = v + sum_z[target]
+    own_x[...] = v
+    for k, target in x_others:
+        begin(s_copy(own_x, sum_x.at[px], 12 + k, sx_recv.at[px], {"patch": w.block(k, 0)}))
+
+
+    q.x_forward()
+    cl.z_relay()
+    o.own_send()
+    o.z_forward(True)
+    q.core_wait(steps=(3, 1))
+    attend(1)
+    attend(2)
 
     v = own_x[...]
     for k, target in x_others:
@@ -447,27 +423,57 @@
     for k, target in z_others:
         begin(s_copy(score.at[pc, pz], score.at[pc, pz], 16 + k, sg_recv.at[pz], {"patch": w.block(0, k)}))
 
+    first(0)
+    cl.own_send()
+    cl.z_forward(True)
+    q.far()
+    q.core_wait(steps=(2,))
+    attend(3)
+
+
+    last = far_y + 1 - tz
+
+    def project(n, count, sources, fresh=False):
+        rows = pl.ds(SEQ * n, SEQ * count)
+        for k, source in enumerate(sources):
+            block = jnp.concatenate([obuf[4 * source + j] for j in range(4)], axis=1)
+            piece = jnp.dot(att[source, rows], block, preferred_element_type=F32)
+            if fresh and k == 0:
+                head[rows] = piece
+            else:
+                head[rows] += piece
+
     first(1)
     first(2)
-    o.far()
-    cl.x_forward(first=0)
+    o.x_near(0)
+    o.x_near(1)
+    second(0)
+
+    o.x_near(2)
+    o.x_near(3)
     first(3)
     for k, target in z_others:
         s_copy(score.at[pc, target], score.at[pc, target], 0, sg_recv.at[target], {"patch": w.block(0, k)}).wait_recv()
     begin(s_copy(score.at[pc], score.at[pc], 20, s_recv.at[9], {"patch": partner}))
-    second(0)
+    second(1)
+    crossed(2)
+    cl.x_forward(first=0)
+
+    o.far()
+    crossed(3)
+    o.core_wait()
+    project(0, 4, (t, beside, up + tz, down + tz), True)
     cl.far()
-    second(1)
-    o.core_wait()
-    project_most(0)
+    crossed(0)
+    crossed(1)
     second(2)
+    second(3)
+    project(0, 4, (far_y + tz, up + 1 - tz, down + 1 - tz))
     s_copy(score.at[pc], score.at[1 - pc], 0, s_recv.at[9], {"patch": partner}).wait_recv()
     score_t[...] = jnp.transpose(score[...].reshape(SCORED, FB).astype(F32)).astype(BF16)
-    project_most(1)
-    second(3)
     cl.core_wait()
 
-    gain = gains_ref[1:]
+    gain = fgain_ref[...].astype(F32).reshape(1, FB)
     share = TOKENS // NT
 
     def l_copy(target, to):
@@ -483,31 +489,36 @@
         )
 
     for n in range(PROMPTS):
-        if n >= 2:
-            project_most(n)
-        third(n)
-        project(n, last)
+        if n == 0:
+            third(0)
+            third(1)
+            project(0, 2, (last,))
+        if n == 2:
+            third(2)
+            third(3)
+            project(2, 2, (last,))
 
         def finish(i, carry, n=n):
             at = pl.ds(pl.multiple_of(SEQ * n + ROWS * i, ROWS), ROWS)
+            token = pl.ds(pl.multiple_of(SEQ * prompts[n] + ROWS * i, ROWS), ROWS)
             local_at = pl.ds(pl.multiple_of(ROWS * i, ROWS), ROWS)
             e = early_ref[local_at, :1] > 0.5
             late = late_ref[local_at, :1] > 0.5
-            v = corrupt_ref[at, :].astype(F32)
-            v = jnp.where(e, cbuf[8 * n + i, 0].astype(F32), v)
-            v = v + head[n, local_at, :]
-            v = jnp.where(late, cbuf[8 * n + i, 1].astype(F32), v)
+            v = corrupt_ref[token, :].astype(F32)
+            v = jnp.where(e, cbuf[8 * prompts[n] + i, 0].astype(F32), v)
+            v = v + head[at, :]
+            v = jnp.where(late, cbuf[8 * prompts[n] + i, 1].astype(F32), v)
             squares[local_at, :] = jnp.broadcast_to(
                 jnp.sum(v * v, axis=1, keepdims=True), (ROWS, 128)
             )
             fin[local_at, :] = (v * gain).astype(BF16)
             return carry
 
-        lax.fori_loop(0, SEQ // ROWS, finish, 0)
-        ssq[n] = jnp.transpose(squares[...])[:8]
+        lax.fori_loop(0, SEQ // ROWS, finish, 0, unroll=4)
+        ssq[prompts[n]] = jnp.transpose(squares[...])[:8]
         value = jnp.dot(fin[...], score_t[...], preferred_element_type=F32).astype(BF16)
         for s in range(2):
-            target = 2 * n + s
+            target = 2 * prompts[n] + s
             lg[target] = value[share * s : share * (s + 1)]
 
             @pl.when(target != t)
@@ -551,7 +562,7 @@
     return pl.pallas_call(
         layer_kernel,
         out_shape=jax.ShapeDtypeStruct((share, SCORED), F32),
-        in_specs=[hbm] * 7 + [smem] + [vmem] * 5,
+        in_specs=[hbm] * 7 + [smem] + [vmem] * 6,
         out_specs=vmem,
         scratch_shapes=[
             pltpu.VMEM((TOKENS, FB), BF16),
@@ -570,7 +581,7 @@
             pltpu.VMEM((NP, FB, 128), BF16),
             pltpu.VMEM((NP, 2, ROWS, FB), BF16),
             pltpu.VMEM((NT, TOKENS, FB), BF16),
-            pltpu.VMEM((PROMPTS, SEQ, FB), F32),
+            pltpu.VMEM((TOKENS, FB), F32),
             pltpu.VMEM((SEQ, SEQ), F32),
             pltpu.VMEM((SEQ, SEQ), F32),
             pltpu.VMEM((NT, SCORED, FB), BF16),
@@ -628,10 +639,9 @@
     w_query, w_key, w_value, w_out, unembed, scored_ids, base_logits,
 ):
     cosine, sine = rope_tables()
-    gains = jnp.stack([norm_gain, final_gain]).astype(F32)
     out = layer(
         resid_corrupt, resid_clean, w_query, w_key, w_value, w_out, unembed,
-        patch_level, patch_mask, scored_ids[None, :], gains, jnp.asarray(cosine), jnp.asarray(sine),
+        patch_level, patch_mask, scored_ids[None, :], norm_gain, final_gain, jnp.asarray(cosine), jnp.asarray(sine),
     )
     return (out - base_logits)[None]
 

time: 119 us -> 105 us (0.88)
  Pallas kernels: 113 us -> 102 us
  local copies, waits for them, and re-layouts: 1.37 us -> 0.01 us
    pallas_call x1, Pallas kernels: 113 us -> 102 us  [layer(): pl.pallas_call(layer_kernel, out_shape=jax.ShapeDtypeStruct((share, SCORE...]
    another operation x2 -> x0, local copies, waits for them, and re-layouts: 1.36 us -> none  [on_device(): gains = jnp.stack([norm_gain, final_gain]).astype(F32)]
where the time goes in v4:
time: 105 us; the launch traced here: 104 us
  Pallas kernels  102 us (97%)
  other arithmetic  1.48 us (1%)
    pallas_call x1, Pallas kernels, layer(): pl.pallas_call(layer_kernel, out_shape=jax.ShapeDtypeStruct((share, SCORE...  102 us

profile of v4, /device:TPU:2, one launch (start us, length us, event | category | flops | bytes accessed | tf_op | source)
XLA Modules:
  0.0 104.0 jit_solution(16502439662649458484)
XLA Ops:
  0.7 0.0 copy-start
  0.7 101.8 %layer.1 = f32[64,256]{1,0:T(8,128)} custom-call(bf16[512,512]{1,0:T(8,128)(2,1)} %corrupt_hbm.1, bf16[2,16,512]{2,1,0:T(8,128)(2,1)} %clean_hbm.1, bf16[128,512]{1,0:T(8,128)(2,1)} %wq_hbm.1, bf16[128,128]{1,0:T(8,128)(2,1)} %wk_hbm.1, bf16[128,128]{1,0:T(8,128)(2,1)} %wv_hbm.1, bf16[512,128]{1,0:T(8,128)(2,1)} %wo_hbm.1, bf16[501,4096]{1,0:T(8,128)(2,1)} %unembed_hbm.1, ...), custom_call_target="tpu_custom_call" | custom-call | flops 4000000000 | bytes 20971520 | tf_op jit(solution)/shard_map/layer/pallas_call | solution.py:562
  102.5 0.0 copy-done
  102.5 1.5 %subtract_bitcast_fusion = f32[1,64,256]{2,1,0:T(8,128)} fusion(f32[64,256]{1,0:T(8,128)} %layer.1, f32[64,256]{1,0:T(8,128)S(1)} %copy-done), kind=kLoop, calls=%fused_computation | loop fusion | flops 16384 | bytes 196608 | tf_op jit(solution)/shard_map/broadcast_in_dim | solution.py:646
Async XLA Ops:
  0.7 101.8 %copy-start = (f32[64,256]{1,0:T(8,128)S(1)}, f32[64,256]{1,0:T(8,128)}, u32[]{:S(2)}) copy-start(f32[64,256]{1,0:T(8,128)} %param.27) | copy-start | bytes 196612

commit v5 on v4

--- a/solution.py
+++ b/solution.py
@@ -123,17 +123,17 @@
     corrupt_hbm, clean_hbm, wq_hbm, wk_hbm, wv_hbm, wo_hbm, unembed_hbm,
     level_ref, mask_ref, ids_ref, ngain_ref, fgain_ref, cos_ref, sin_ref,
     out_ref,
-    corrupt_ref, clean_ref, w_ref, wo_ref, wo_own, unembed_ref,
-    xin, xrecv, nbuf, wbuf, acc, qown, qbuf, obuf, cbuf, att, head, early_ref, late_ref,
+    corrupt_ref, clean_ref, wo_ref, wo_own, unembed_ref,
+    x_own, x_sum, x_got, nsend, ngot, wbuf, acc, pbuf, pgot, qown, qbuf, obuf, cbuf, att, head, early_ref, late_ref,
     chosen, chosen_got, paired, spread, mine, mine_got, spread_z, sum_z, sum_x, own_x, score, fin, score_t, squares, ssq, ssq_got, lg, lg_got,
-    local, x_send, x_recv, w_send, w_recv, q_send, q_recv, o_send, o_recv, c_send, c_recv, a_send, a_recv,
+    local, x_send, x_recv, v_send, v_recv, p_send, p_recv, w_send, w_recv, q_send, q_recv, o_send, o_recv, c_send, c_recv, a_send, a_recv,
     s_send, s_recv, sz_recv, sx_recv, sg_recv, l_send, l_recv, n_send, n_recv,
 ):
     t = lax.axis_index("tp")
-    w = PatchGather(w_ref, wbuf, w_send, w_recv)
     q = PatchGather(qown, qbuf, q_send, q_recv)
     o = PatchGather(wo_own, obuf, o_send, o_recv)
     cl = PatchGather(clean_ref, cbuf, c_send, c_recv)
+    w = q
     me, px, pz, pc = w.me, w.x, w.z, w.c
     ty, tz = t // 2, t % 2
     beside = t + 1 - 2 * tz
@@ -150,9 +150,9 @@
             [
                 (corrupt_hbm, corrupt_ref),
                 (clean_hbm, clean_ref),
-                (wq_hbm, w_ref.at[:, pl.ds(0, QCOLS)]),
-                (wk_hbm, w_ref.at[:, pl.ds(QCOLS, KVCOL)]),
-                (wv_hbm, w_ref.at[:, pl.ds(QCOLS + KVCOL, KVCOL)]),
+                (wq_hbm, wbuf.at[2 * px + pc, :, pl.ds(0, QCOLS)]),
+                (wk_hbm, wbuf.at[2 * px + pc, :, pl.ds(QCOLS, KVCOL)]),
+                (wv_hbm, wbuf.at[2 * px + pc, :, pl.ds(QCOLS + KVCOL, KVCOL)]),
                 (wo_hbm, wo_ref),
                 (unembed_hbm, unembed_ref),
             ]
@@ -166,6 +166,7 @@
         + [{"patch": w.block(0, dz)} for dz in (1, 3, 2)]
         + [{"patch": w.block(dx, 0)} for dx in (1, 3, 2)]
         + [{"patch": partner}]
+        + [{"patch": w.block(0, dz), "tp": k} for dz in (1, 3, 2) for k in others]
     )
     for peer in peers:
         pl.semaphore_signal(barrier, inc=1, device_id=peer, device_id_type=MESH)
@@ -178,10 +179,10 @@
 
     for c in loads[:2]:
         c.wait()
-    xin[:ROWS] = corrupt_ref[pl.ds(pl.multiple_of(me * ROWS, ROWS), ROWS), :]
-    xin[ROWS : 2 * ROWS] = clean_ref[0]
-    xin[2 * ROWS :] = jnp.broadcast_to(ngain_ref[...].astype(F32).reshape(1, FB), (ROWS, FB)).astype(BF16)
-    xrecv[t] = xin[...]
+    x_own[:ROWS] = corrupt_ref[pl.ds(pl.multiple_of(me * ROWS, ROWS), ROWS), :].astype(F32)
+    x_own[ROWS:] = clean_ref[0].astype(F32)
+    v = x_own[...]
+    x_sum[...] = jnp.broadcast_to(jnp.sum(v * v, axis=1, keepdims=True), (2 * ROWS, 128))
     spliced = jnp.transpose(jnp.broadcast_to(mask_ref[...].astype(F32), (SEQ, SEQ)))
     level = level_ref[0].astype(F32)
     early_ref[...] = spliced * (1.0 - level)
@@ -199,8 +200,27 @@
 
     def x_copy(k, target, to):
         return pltpu.make_async_remote_copy(
-            src_ref=xin, dst_ref=xrecv.at[to], send_sem=x_send.at[k], recv_sem=x_recv.at[to],
+            src_ref=x_sum, dst_ref=x_got.at[to], send_sem=x_send.at[k], recv_sem=x_recv.at[to],
             device_id={"tp": target}, device_id_type=MESH,
+        )
+
+    def v_copy(h, k, x, z, where):
+        return pltpu.make_async_remote_copy(
+            src_ref=nsend.at[h], dst_ref=ngot.at[x, z], send_sem=v_send.at[h, k], recv_sem=v_recv.at[x, z],
+            device_id=where, device_id_type=MESH,
+        )
+
+    def p_copy(k, source, to):
+        return pltpu.make_async_remote_copy(
+            src_ref=pbuf.at[source], dst_ref=pgot.at[to], send_sem=p_send.at[k], recv_sem=p_recv.at[to],
+            device_id={"patch": w.block(0, k)}, device_id_type=MESH,
+        )
+
+    def w_copy(slot, dx, c, target):
+        index = 2 * ((px + dx + 4) % 4) + c
+        return pltpu.make_async_remote_copy(
+            src_ref=wbuf.at[index], dst_ref=wbuf.at[index], send_sem=w_send.at[slot], recv_sem=w_recv.at[index],
+            device_id={"patch": target}, device_id_type=MESH,
         )
 
     def s_copy(src, dst, send, recv, where):
@@ -209,10 +229,11 @@
             device_id=where, device_id_type=MESH,
         )
 
-    w.z_send()
-    w.own_send()
     for k, target in enumerate(others):
         begin(x_copy(k, target, t))
+    begin(w_copy(0, 0, pc, w.block(1, 0)))
+    begin(w_copy(1, 0, pc, w.block(3, 0)))
+    begin(w_copy(2, 0, pc, partner))
     swap = s_copy(wo_ref, wo_own, 21, s_recv.at[10], {"patch": swap_p, "tp": swap_t})
 
     @pl.when(swaps)
@@ -236,6 +257,48 @@
         chosen_got, 0, s_recv.at[0], {"patch": partner},
     )
     begin(pair)
+
+    total = x_sum[...]
+    for target in others:
+        x_copy(0, target, target).wait_recv()
+        total = total + x_got[target]
+    scale = lax.rsqrt(total[:, :1] / D + EPSILON)
+    v = (x_own[...] * scale * ngain_ref[...].astype(F32).reshape(1, FB)).astype(BF16)
+    halves = []
+    for h in range(2):
+        nsend[h] = v[:, 256 * h : 256 * (h + 1)]
+    for h in range(2):
+        z_to = 2 * tz + h
+        for k in range(NT):
+            c = v_copy(h, k, ty, pz, {"patch": 8 * px + 2 * z_to + pc, "tp": (t + k) % NT})
+            if k > 0:
+                begin(c)
+            else:
+                halves.append((z_to, c))
+
+                @pl.when(z_to != pz)
+                def _(c=c):
+                    c.start()
+
+    @pl.when(pz // 2 == tz)
+    def _():
+        ngot[ty, pz] = nsend[pz % 2]
+
+    w_copy(0, -w.way, pc, partner).wait_recv()
+    begin(w_copy(3, -w.way, pc, w.block(w.way, 0)))
+    begin(w_copy(4, -w.way, pc, partner))
+    w_copy(0, w.way, pc, partner).wait_recv()
+    begin(w_copy(5, w.way, pc, partner))
+
+    @pl.when(swaps)
+    def _():
+        swap.wait_recv()
+
+    @pl.when(jnp.logical_not(swaps))
+    def _():
+        wo_own[...] = wo_ref[...]
+
+    o.z_send()
     pair.wait_recv()
     paired[...] = (
         chosen[:, pl.ds(pl.multiple_of(half * pc, half), half)] + chosen_got[...]
@@ -244,31 +307,38 @@
     for k, y in y_others:
         begin(s_copy(paired.at[y], spread.at[ty], k, s_recv.at[1 + ty], {"tp": 2 * y + tz}))
 
-    w.x_near(0)
-    w.z_forward()
-
-    @pl.when(swaps)
-    def _():
-        swap.wait_recv()
-
-    @pl.when(jnp.logical_not(swaps))
-    def _():
-        wo_own[...] = wo_ref[...]
-
-    o.z_send()
-    for target in others:
-        x_copy(0, target, target).wait_recv()
-    total = jnp.zeros((2 * ROWS, 1), F32)
-    for k in range(NT):
-        v = xrecv[k, : 2 * ROWS, :].astype(F32)
-        total = total + jnp.sum(v * v, axis=1, keepdims=True)
-    scale = lax.rsqrt(total / D + EPSILON)
-    for k in range(NT):
-        v = xrecv[k, : 2 * ROWS, :].astype(F32)
-        g = xrecv[k, 2 * ROWS :, :].astype(F32)[:1]
-        v = (v * scale * g).astype(BF16)
-        for j in range(4):
-            nbuf[4 * k + j] = v[:, 128 * j : 128 * (j + 1)]
+    w_copy(0, 2, pc, partner).wait_recv()
+    begin(w_copy(6, 2, pc, partner))
+    for kz in range(4):
+        z_from = (pz + kz) % 4
+        for x in range(4):
+            t_from = 2 * x + pz // 2
+            c = v_copy(0, 0, x, z_from, {"patch": partner})
+            if kz > 0:
+                c.wait_recv()
+            else:
+
+                @pl.when(t_from != t)
+                def _(c=c):
+                    c.wait_recv()
+
+    for dx in range(4):
+        w_copy(0, dx, 1 - pc, partner).wait_recv()
+    for x in range(4):
+        piece = jnp.dot(
+            ngot[x].reshape(8 * ROWS, 256), wbuf[2 * x : 2 * x + 2].reshape(256, WCOLS),
+            preferred_element_type=F32,
+        )
+        if x == 0:
+            acc[...] = piece
+        else:
+            acc[...] += piece
+    pbuf[...] = acc[...].astype(BF16).reshape(4, 2 * ROWS, WCOLS)
+    for k, target in z_others:
+        begin(p_copy(k, target, pz))
+    o.z_relay()
+    o.own_send()
+    obuf[me] = wo_own[...]
 
     v = paired[ty]
     for k, y in y_others:
@@ -277,31 +347,16 @@
     mine[...] = v
     begin(s_copy(mine.at[1 - tz], mine_got, 4, s_recv.at[5], {"tp": beside}))
 
-    acc[...] = jnp.dot(nbuf[me], w_ref[...], preferred_element_type=F32)
-
-    def add(b):
-        acc[...] += jnp.dot(nbuf[b], wbuf[b], preferred_element_type=F32)
-
-    for b in [w.block(0, dz) for dz in (3, 1, 2)] + [w.block(dx, 0) for dx in (3, 1)]:
-        add(b)
-    w.x_forward(add)
-    obuf[me] = wo_own[...]
-    o.z_relay()
-    cl.z_send()
-
-    s_copy(mine.at[1 - tz], mine_got, 4, s_recv.at[5], {"tp": beside}).wait_recv()
-    spread_z[...] = (mine[tz] + mine_got[...]).reshape(4, half // 4, FB)
+    full = acc[pl.ds(pl.multiple_of(2 * ROWS * pz, 2 * ROWS), 2 * ROWS), :]
     for k, target in z_others:
-        begin(s_copy(spread_z.at[target], sum_z.at[pz], 8 + k, sz_recv.at[pz], {"patch": w.block(0, k)}))
-
-    w.far(add)
-    w.core_wait(add)
+        p_copy(k, target, target).wait_recv()
+        full = full + pgot[target].astype(F32)
 
     at = pl.ds(pl.multiple_of((me * ROWS) % SEQ, ROWS), ROWS)
     cosine = jnp.concatenate([cos_ref[at, :]] * 2, axis=0)
     sine = jnp.concatenate([sin_ref[at, :]] * 2, axis=0)
     for h in range(WCOLS // HD):
-        v = acc[:, HD * h : HD * (h + 1)]
+        v = full[:, HD * h : HD * (h + 1)]
         if h < 5:
             v = v * cosine + pltpu.roll(v, HD // 2, 1) * sine
         v = v.astype(BF16)
@@ -310,6 +365,8 @@
     qbuf[me] = qown[...]
     q.z_send()
     q.own_send()
+    cl.z_send()
+    o.z_forward(True)
 
     early = early_ref[...] > 0.5
     row = lax.broadcasted_iota(jnp.int32, (4 * SEQ, SEQ), 0) % SEQ
@@ -398,6 +455,18 @@
     q.core_wait(steps=(0,))
     attend(0)
 
+    s_copy(mine.at[1 - tz], mine_got, 4, s_recv.at[5], {"tp": beside}).wait_recv()
+    spread_z[...] = (mine[tz] + mine_got[...]).reshape(4, half // 4, FB)
+    for k, target in z_others:
+        begin(s_copy(spread_z.at[target], sum_z.at[pz], 8 + k, sz_recv.at[pz], {"patch": w.block(0, k)}))
+
+    cl.z_relay()
+    q.x_forward()
+    o.x_near(0)
+    q.core_wait(steps=(3, 1))
+    attend(1)
+    attend(2)
+
     v = spread_z[pz]
     for k, target in z_others:
         s_copy(spread_z.at[target], sum_z.at[target], 0, sz_recv.at[target], {"patch": w.block(0, k)}).wait_recv()
@@ -406,14 +475,13 @@
     for k, target in x_others:
         begin(s_copy(own_x, sum_x.at[px], 12 + k, sx_recv.at[px], {"patch": w.block(k, 0)}))
 
-
-    q.x_forward()
-    cl.z_relay()
-    o.own_send()
-    o.z_forward(True)
-    q.core_wait(steps=(3, 1))
-    attend(1)
-    attend(2)
+    first(0)
+    cl.own_send()
+    cl.z_forward(True)
+    q.far()
+    q.core_wait(steps=(2,))
+    attend(3)
+    o.x_near(1)
 
     v = own_x[...]
     for k, target in x_others:
@@ -422,14 +490,6 @@
     score[pc, pz] = v
     for k, target in z_others:
         begin(s_copy(score.at[pc, pz], score.at[pc, pz], 16 + k, sg_recv.at[pz], {"patch": w.block(0, k)}))
-
-    first(0)
-    cl.own_send()
-    cl.z_forward(True)
-    q.far()
-    q.core_wait(steps=(2,))
-    attend(3)
-
 
     last = far_y + 1 - tz
 
@@ -445,8 +505,6 @@
 
     first(1)
     first(2)
-    o.x_near(0)
-    o.x_near(1)
     second(0)
 
     o.x_near(2)
@@ -545,9 +603,15 @@
     def _():
         swap.wait_send()
 
+    for z_to, c in halves:
+
+        @pl.when(z_to != pz)
+        def _(c=c):
+            c.wait_send()
+
     for c in started:
         c.wait_send()
-    for g in (w, q, o, cl):
+    for g in (q, o, cl):
         g.drain()
 
 
@@ -567,15 +631,18 @@
         scratch_shapes=[
             pltpu.VMEM((TOKENS, FB), BF16),
             pltpu.VMEM((2, ROWS, FB), BF16),
-            pltpu.VMEM((128, WCOLS), BF16),
             pltpu.VMEM((FB, 128), BF16),
             pltpu.VMEM((FB, 128), BF16),
             pltpu.VMEM((rows_dev, D), BF16),
-            pltpu.VMEM((3 * ROWS, FB), BF16),
-            pltpu.VMEM((NT, 3 * ROWS, FB), BF16),
-            pltpu.VMEM((NP, 2 * ROWS, 128), BF16),
-            pltpu.VMEM((NP, 128, WCOLS), BF16),
-            pltpu.VMEM((2 * ROWS, WCOLS), F32),
+            pltpu.VMEM((2 * ROWS, FB), F32),
+            pltpu.VMEM((2 * ROWS, 128), F32),
+            pltpu.VMEM((NT, 2 * ROWS, 128), F32),
+            pltpu.VMEM((2, 2 * ROWS, 256), BF16),
+            pltpu.VMEM((4, 4, 2 * ROWS, 256), BF16),
+            pltpu.VMEM((8, 128, WCOLS), BF16),
+            pltpu.VMEM((8 * ROWS, WCOLS), F32),
+            pltpu.VMEM((4, 2 * ROWS, WCOLS), BF16),
+            pltpu.VMEM((4, 2 * ROWS, WCOLS), BF16),
             pltpu.VMEM((2, ROWS, WCOLS), BF16),
             pltpu.VMEM((NP, 2, ROWS, WCOLS), BF16),
             pltpu.VMEM((NP, FB, 128), BF16),
@@ -604,7 +671,9 @@
             pltpu.VMEM((NT, share, SCORED), BF16),
             dma((7,)),
             dma((NT,)), dma((NT,)),
-            dma((N_SENDS,)), dma((NP,)),
+            dma((2, NT)), dma((4, 4)),
+            dma((4,)), dma((4,)),
+            dma((7,)), dma((8,)),
             dma((N_SENDS,)), dma((NP,)),
             dma((N_SENDS,)), dma((NP,)),
             dma((N_SENDS,)), dma((NP,)),

time: 105 us -> 99.5 us (0.948)
  Pallas kernels: 102 us -> 95.7 us
    pallas_call x1, Pallas kernels: 102 us -> 95.7 us  [layer(): pl.pallas_call(layer_kernel, out_shape=jax.ShapeDtypeStruct((share, SCORE...]
where the time goes in v5:
time: 99.5 us; the launch traced here: 97.9 us
  Pallas kernels  95.7 us (96%)
  other arithmetic  1.48 us (1%)
    pallas_call x1, Pallas kernels, layer(): pl.pallas_call(layer_kernel, out_shape=jax.ShapeDtypeStruct((share, SCORE...  95.7 us

profile of v5, /device:TPU:2, one launch (start us, length us, event | category | flops | bytes accessed | tf_op | source)
XLA Modules:
  0.0 97.9 jit_solution(15724559580676913822)
XLA Ops:
  0.7 0.0 copy-start
  0.7 95.7 %layer.1 = f32[64,256]{1,0:T(8,128)} custom-call(bf16[512,512]{1,0:T(8,128)(2,1)} %corrupt_hbm.1, bf16[2,16,512]{2,1,0:T(8,128)(2,1)} %clean_hbm.1, bf16[128,512]{1,0:T(8,128)(2,1)} %wq_hbm.1, bf16[128,128]{1,0:T(8,128)(2,1)} %wk_hbm.1, bf16[128,128]{1,0:T(8,128)(2,1)} %wv_hbm.1, bf16[512,128]{1,0:T(8,128)(2,1)} %wo_hbm.1, bf16[501,4096]{1,0:T(8,128)(2,1)} %unembed_hbm.1, ...), custom_call_target="tpu_custom_call" | custom-call | flops 4000000000 | bytes 20971520 | tf_op jit(solution)/shard_map/layer/pallas_call | solution.py:626
  96.4 0.0 copy-done
  96.4 1.5 %subtract_bitcast_fusion = f32[1,64,256]{2,1,0:T(8,128)} fusion(f32[64,256]{1,0:T(8,128)} %layer.1, f32[64,256]{1,0:T(8,128)S(1)} %copy-done), kind=kLoop, calls=%fused_computation | loop fusion | flops 16384 | bytes 196608 | tf_op jit(solution)/shard_map/broadcast_in_dim | solution.py:715
Async XLA Ops:
  0.7 95.7 %copy-start = (f32[64,256]{1,0:T(8,128)S(1)}, f32[64,256]{1,0:T(8,128)}, u32[]{:S(2)}) copy-start(f32[64,256]{1,0:T(8,128)} %param.27) | copy-start | bytes 196612

commit v6 on v5

--- a/solution.py
+++ b/solution.py
@@ -340,12 +340,6 @@
     o.own_send()
     obuf[me] = wo_own[...]
 
-    v = paired[ty]
-    for k, y in y_others:
-        s_copy(paired.at[y], spread.at[y], 0, s_recv.at[1 + y], {"tp": 2 * y + tz}).wait_recv()
-        v = v + spread[y]
-    mine[...] = v
-    begin(s_copy(mine.at[1 - tz], mine_got, 4, s_recv.at[5], {"tp": beside}))
 
     full = acc[pl.ds(pl.multiple_of(2 * ROWS * pz, 2 * ROWS), 2 * ROWS), :]
     for k, target in z_others:
@@ -366,6 +360,12 @@
     q.z_send()
     q.own_send()
     cl.z_send()
+    v = paired[ty]
+    for k, y in y_others:
+        s_copy(paired.at[y], spread.at[y], 0, s_recv.at[1 + y], {"tp": 2 * y + tz}).wait_recv()
+        v = v + spread[y]
+    mine[...] = v
+    begin(s_copy(mine.at[1 - tz], mine_got, 4, s_recv.at[5], {"tp": beside}))
     o.z_forward(True)
 
     early = early_ref[...] > 0.5
@@ -510,15 +510,15 @@
     o.x_near(2)
     o.x_near(3)
     first(3)
+    second(1)
+    crossed(2)
+    cl.x_forward(first=0)
+
+    o.far()
+    crossed(3)
     for k, target in z_others:
         s_copy(score.at[pc, target], score.at[pc, target], 0, sg_recv.at[target], {"patch": w.block(0, k)}).wait_recv()
     begin(s_copy(score.at[pc], score.at[pc], 20, s_recv.at[9], {"patch": partner}))
-    second(1)
-    crossed(2)
-    cl.x_forward(first=0)
-
-    o.far()
-    crossed(3)
     o.core_wait()
     project(0, 4, (t, beside, up + tz, down + tz), True)
     cl.far()

time: 99.5 us -> 98.6 us (level)
  no operation moved by 1% of the time
where the time goes in v6:
time: 98.6 us; the launch traced here: 97.3 us
  Pallas kernels  95.1 us (96%)
  other arithmetic  1.48 us (2%)
    pallas_call x1, Pallas kernels, layer(): pl.pallas_call(layer_kernel, out_shape=jax.ShapeDtypeStruct((share, SCORE...  95.1 us

profile of v6, /device:TPU:2, one launch (start us, length us, event | category | flops | bytes accessed | tf_op | source)
XLA Modules:
  0.0 97.3 jit_solution(9089737220636291578)
XLA Ops:
  0.7 0.0 copy-start
  0.7 95.1 %layer.1 = f32[64,256]{1,0:T(8,128)} custom-call(bf16[512,512]{1,0:T(8,128)(2,1)} %corrupt_hbm.1, bf16[2,16,512]{2,1,0:T(8,128)(2,1)} %clean_hbm.1, bf16[128,512]{1,0:T(8,128)(2,1)} %wq_hbm.1, bf16[128,128]{1,0:T(8,128)(2,1)} %wk_hbm.1, bf16[128,128]{1,0:T(8,128)(2,1)} %wv_hbm.1, bf16[512,128]{1,0:T(8,128)(2,1)} %wo_hbm.1, bf16[501,4096]{1,0:T(8,128)(2,1)} %unembed_hbm.1, ...), custom_call_target="tpu_custom_call" | custom-call | flops 4000000000 | bytes 20971520 | tf_op jit(solution)/shard_map/layer/pallas_call | solution.py:626
  95.8 0.0 copy-done
  95.8 1.5 %subtract_bitcast_fusion = f32[1,64,256]{2,1,0:T(8,128)} fusion(f32[64,256]{1,0:T(8,128)} %layer.1, f32[64,256]{1,0:T(8,128)S(1)} %copy-done), kind=kLoop, calls=%fused_computation | loop fusion | flops 16384 | bytes 196608 | tf_op jit(solution)/shard_map/broadcast_in_dim | solution.py:715
Async XLA Ops:
  0.7 95.1 %copy-start = (f32[64,256]{1,0:T(8,128)S(1)}, f32[64,256]{1,0:T(8,128)}, u32[]{:S(2)}) copy-start(f32[64,256]{1,0:T(8,128)} %param.27) | copy-start | bytes 196612

commit v7 on v6

--- a/solution.py
+++ b/solution.py
@@ -546,7 +546,7 @@
             device_id={"tp": target}, device_id_type=MESH,
         )
 
-    for n in range(PROMPTS):
+    for n in (2, 3, 0, 1):
         if n == 0:
             third(0)
             third(1)

time: 98.6 us -> 97.6 us (0.990); the launches traced: 97.3 us -> 97.3 us
  no operation moved by 1% of the time
where the time goes in v7:
time: 97.6 us; the launch traced here: 97.3 us
  Pallas kernels  95.1 us (97%)
  other arithmetic  1.48 us (2%)
    pallas_call x1, Pallas kernels, layer(): pl.pallas_call(layer_kernel, out_shape=jax.ShapeDtypeStruct((share, SCORE...  95.1 us

profile of v7, /device:TPU:2, one launch (start us, length us, event | category | flops | bytes accessed | tf_op | source)
XLA Modules:
  0.0 97.3 jit_solution(16022560929521884812)
XLA Ops:
  0.7 0.0 copy-start
  0.7 95.1 %layer.1 = f32[64,256]{1,0:T(8,128)} custom-call(bf16[512,512]{1,0:T(8,128)(2,1)} %corrupt_hbm.1, bf16[2,16,512]{2,1,0:T(8,128)(2,1)} %clean_hbm.1, bf16[128,512]{1,0:T(8,128)(2,1)} %wq_hbm.1, bf16[128,128]{1,0:T(8,128)(2,1)} %wk_hbm.1, bf16[128,128]{1,0:T(8,128)(2,1)} %wv_hbm.1, bf16[512,128]{1,0:T(8,128)(2,1)} %wo_hbm.1, bf16[501,4096]{1,0:T(8,128)(2,1)} %unembed_hbm.1, ...), custom_call_target="tpu_custom_call" | custom-call | flops 4000000000 | bytes 20971520 | tf_op jit(solution)/shard_map/layer/pallas_call | solution.py:626
  95.8 0.0 copy-done
  95.8 1.5 %subtract_bitcast_fusion = f32[1,64,256]{2,1,0:T(8,128)} fusion(f32[64,256]{1,0:T(8,128)} %layer.1, f32[64,256]{1,0:T(8,128)S(1)} %copy-done), kind=kLoop, calls=%fused_computation | loop fusion | flops 16384 | bytes 196608 | tf_op jit(solution)/shard_map/broadcast_in_dim | solution.py:715
Async XLA Ops:
  0.7 95.1 %copy-start = (f32[64,256]{1,0:T(8,128)S(1)}, f32[64,256]{1,0:T(8,128)}, u32[]{:S(2)}) copy-start(f32[64,256]{1,0:T(8,128)} %param.27) | copy-start | bytes 196612
